TPU v7x, 256 devices: a whole 4x4x8 slice. The times are simulated.
256 devices in a mesh: fsdp: 64 (over y, z, x_lo), tp: 4 (over x_hi, core).
Axes of the slice: x: 4 (x_hi: 2, x_lo: 2; x = x_hi * 2 + x_lo), y: 4, z: 8, core: 2. Of those that a mesh axis runs over, the one named last changes fastest.
Arguments:
- tokens: bfloat16 [24576, 5632], P('fsdp', 'tp'), may hold values from -6 to 6
- gain: float32 [5632], replicated, may hold values from 0.1 to 1.9
- query_projection_weight: bfloat16 [5632, 6144], P('fsdp', 'tp'), may hold values from -0.078125 to 0.078125
- key_projection_weight: bfloat16 [5632, 1024], P('fsdp', 'tp'), may hold values from -0.078125 to 0.078125
- value_projection_weight: bfloat16 [5632, 1024], P('fsdp', 'tp'), may hold values from -0.078125 to 0.078125
- adapter_down_factors: bfloat16 [3, 16, 5632], replicated, may hold values from -0.078125 to 0.078125
- query_adapter_up: bfloat16 [16, 6144], P(None, 'tp'), may hold values from -0.078125 to 0.078125
- key_adapter_up: bfloat16 [16, 1024], P(None, 'tp'), may hold values from -0.1875 to 0.1875
- value_adapter_up: bfloat16 [16, 1024], P(None, 'tp'), may hold values from -0.1875 to 0.1875
- query_cotangent: bfloat16 [24576, 6144], P('fsdp', 'tp'), may hold values from -6 to 6
- key_cotangent: bfloat16 [24576, 1024], P('fsdp', 'tp'), may hold values from -6 to 6
- value_cotangent: bfloat16 [24576, 1024], P('fsdp', 'tp'), may hold values from -6 to 6
Outputs:
- grad_tokens: bfloat16 [24576, 5632], P('fsdp', 'tp')
- grad_down: float32 [3, 16, 5632], P(None, None, 'tp')
- grad_up_query: float32 [16, 6144], P(None, 'tp')
- grad_up_key: float32 [16, 1024], P(None, 'tp')
- grad_up_value: float32 [16, 1024], P(None, 'tp')
All inputs are finite; a program needn't handle non-finite values.
Results may differ from a plain program's by a relative error of at most 0.0096.
Values may be sent and summed in bfloat16 or wider, within the bound.
A program may use at most 128 MiB of HBM per device.

v0:
```python
import math

import jax
import jax.numpy as jnp
from jax import lax
from jax.sharding import PartitionSpec as P

norm_eps = 1e-05
adapter_scale = 2.0


def from_everyone(array, axis):
    copies = jnp.broadcast_to(array, (lax.axis_size(axis), *array.shape))
    return lax.all_to_all(copies, axis, split_axis=0, concat_axis=0, tiled=True)


def over_copies(array, axis):
    return from_everyone(array, axis).sum(axis=0)


def in_one(arrays, axis):
    ends = [0]
    for a in arrays:
        ends.append(ends[-1] + a.size)
    total = over_copies(jnp.concatenate([a.ravel() for a in arrays]), axis)
    return tuple((total[b:e].reshape(a.shape) for a, b, e in zip(arrays, ends, ends[1:])))


def in_blocks(array, dim, count):
    before, after = (array.shape[:dim], array.shape[dim + 1 :])
    return jnp.moveaxis(array.reshape(*before, count, -1, *after), dim, 0)


def sum_at_owner(array, axis, dim):
    count = lax.axis_size(axis)
    pieces = lax.all_to_all(in_blocks(array, dim, count), axis, 0, 0, tiled=True)
    return jnp.sum(pieces, axis=0)


def filled_up(lines, count):
    spare = -lines.shape[0] % count
    if not spare:
        return lines
    return jnp.concatenate([lines, jnp.zeros((spare, *lines.shape[1:]), lines.dtype)])


def joined_along(pieces, dim):
    lengths = list(pieces.shape[1:])
    lengths[dim] *= pieces.shape[0]
    return jnp.moveaxis(pieces, 0, dim).reshape(lengths)


def gathered_copies(array, axis, dim):
    return joined_along(from_everyone(array, axis), dim)


def sum_by_parts(array, axes):
    own = sum_at_owner(filled_up(array, lax.axis_size(axes)), axes, 0)
    whole = gathered_copies(own, axes, 0)
    return whole[: len(array)].reshape(array.shape)


def packed_total(arrays, axis):
    line, at, done = (jnp.concatenate([a.reshape(-1) for a in arrays]), 0, [])
    total = sum_by_parts(line, axis)
    for a in arrays:
        done.append(total[at : at + a.size].reshape(a.shape))
        at += a.size
    return tuple(done)


def in_one_piece(arrays, axis, dim, along):
    widths = [a.shape[along] for a in arrays]
    both = jnp.concatenate(arrays, axis=along)
    whole = lax.all_gather(both, axis, axis=dim, tiled=True)
    return tuple(jnp.split(whole, [sum(widths[:k]) for k in range(1, len(widths))], axis=along))


def transposed_product(cotangent, piece):
    return lax.dot_general(
        cotangent, piece, (((1,), (1,)), ((), ())), preferred_element_type=jnp.float32
    )


def shards(
    tokens,
    gain,
    query_projection_weight,
    key_projection_weight,
    value_projection_weight,
    adapter_down_factors,
    query_adapter_up,
    key_adapter_up,
    value_adapter_up,
    query_cotangent,
    key_cotangent,
    value_cotangent,
):
    adapter_up_factors = (query_adapter_up, key_adapter_up, value_adapter_up)
    cotangent_list = (query_cotangent, key_cotangent, value_cotangent)
    tensor_slice_index = lax.axis_index("tp")
    number_of_rows, owned_width = tokens.shape
    full_width = gain.shape[0]
    token_width_matrix = tokens.astype(jnp.float32)
    gain_own = lax.dynamic_slice_in_dim(gain, tensor_slice_index * owned_width, owned_width, 0)
    down_owned_slice = lax.dynamic_slice_in_dim(
        adapter_down_factors, tensor_slice_index * owned_width, owned_width, 2
    )
    scaled_part = token_width_matrix * gain_own[None, :]
    adapter_input_slice = jnp.einsum(
        "td,krd->ktr",
        scaled_part,
        down_owned_slice.astype(jnp.float32),
        precision=lax.Precision.HIGHEST,
    )
    adapter_output_slice = jnp.stack(
        [
            jnp.dot(
                cotangent_list[slice_member],
                adapter_up_factors[slice_member].T,
                preferred_element_type=jnp.float32,
            )
            for slice_member in range(3)
        ]
    )
    squared_total, adapter_input_unnormed, adapter_output = in_one(
        (
            jnp.sum(token_width_matrix * token_width_matrix, axis=1),
            adapter_input_slice,
            adapter_output_slice,
        ),
        "tp",
    )
    inverse_root_mean = lax.rsqrt(squared_total / full_width + norm_eps)[:, None]
    adapter_input = adapter_input_unnormed * inverse_root_mean[None]
    unit_rows = token_width_matrix * inverse_root_mean
    normed = (unit_rows * gain_own[None, :]).astype(jnp.bfloat16)
    input_lowrank = adapter_input.astype(jnp.bfloat16)
    output_lowrank = adapter_output.astype(jnp.bfloat16)
    gradient_scale = adapter_scale / math.sqrt(number_of_rows * lax.axis_size("fsdp"))
    down_local = gradient_scale * jnp.einsum(
        "ktr,td->krd", output_lowrank, normed, preferred_element_type=jnp.float32
    )
    up_local = tuple(
        (
            gradient_scale
            * jnp.dot(
                input_lowrank[slice_member].T,
                cotangent_list[slice_member],
                preferred_element_type=jnp.float32,
            )
            for slice_member in range(3)
        )
    )
    grad_down, grad_up_query, grad_up_key, grad_up_value = packed_total(
        (down_local, up_local[0], up_local[1], up_local[2]), "fsdp"
    )
    pieces = in_one_piece(
        (query_projection_weight, key_projection_weight, value_projection_weight), "fsdp", 0, 1
    )
    block = (
        transposed_product(query_cotangent, pieces[0])
        + transposed_product(key_cotangent, pieces[1])
        + transposed_product(value_cotangent, pieces[2])
    )
    backward_result = lax.psum_scatter(
        block.astype(jnp.bfloat16), "tp", scatter_dimension=1, tiled=True
    ).astype(jnp.float32)
    backward_result = backward_result + adapter_scale * jnp.einsum(
        "ktr,krd->td", output_lowrank, down_owned_slice, preferred_element_type=jnp.float32
    )
    gained = gain_own[None, :] * backward_result
    inner = over_copies(jnp.sum(gained * unit_rows, axis=1), "tp") / full_width
    grad_tokens = (inverse_root_mean * (gained - unit_rows * inner[:, None])).astype(jnp.bfloat16)
    return (grad_tokens, grad_down, grad_up_query, grad_up_key, grad_up_value)


def solution(mesh):
    in_specs = (
        P("fsdp", "tp"),
        P(),
        P("fsdp", "tp"),
        P("fsdp", "tp"),
        P("fsdp", "tp"),
        P(),
        P(None, "tp"),
        P(None, "tp"),
        P(None, "tp"),
        P("fsdp", "tp"),
        P("fsdp", "tp"),
        P("fsdp", "tp"),
    )
    out_specs = (P("fsdp", "tp"), P(None, None, "tp"), P(None, "tp"), P(None, "tp"), P(None, "tp"))
    return jax.shard_map(shards, mesh=mesh, in_specs=in_specs, out_specs=out_specs, check_vma=False)
```

profile of v0, /device:TPU:1, one launch (start us, length us, event | category | flops | bytes accessed | tf_op | source)
XLA Modules:
  0.0 638.0 jit_solution(4544040421141524299)
XLA Ops:
  7.2 0.0 all-gather.2.cloned.1.call-start
  7.2 1.9 pad_maximum_fusion.1
  9.1 0.0 all-gather.2.cloned.1.call-update
  9.1 0.0 reduce-scatter.2.cloned.1.call-start
  9.2 509.6 %all-gather.2.cloned.1.call-done = bf16[5632,2048]{1,0:T(8,128)(2,1)} async-done(((bf16[88,2048]{1,0:T(8,128)(2,1)}), bf16[5632,2048]{1,0:T(8,128)(2,1)}) %all-gather.2.cloned.1.call-update) | async-done | bytes 23068688 | tf_op jit(solution)/shard_map/all_gather | solution.py:75
  518.8 12.5 %fusion = f32[5632,384]{1,0:T(8,128)S(1)} fusion(bf16[384,1536]{1,0:T(8,128)(2,1)S(1)} %copy-done, bf16[5632,2048]{1,0:T(8,128)(2,1)} %all-gather.2.cloned.1.call-done), kind=kOutput, calls=%fused_computation | convolution fusion | flops 6643777536 | bytes 27131904 | tf_op jit(solution)/shard_map/dot_general | solution.py:80
  531.4 3.5 convolution_add_fusion.1
  534.9 5.6 fusion.3
  540.6 2.2 copy.49
  542.8 0.2 convolution_bitcast_fusion.1
  542.9 0.2 convolution_bitcast_fusion.2
  543.1 0.5 convolution_bitcast_fusion.3
  543.6 0.2 copy.52
  543.9 0.2 reshape.72
  544.1 0.8 dynamic_slice.7
  544.9 2.0 fusion.21
  546.8 0.2 copy.51
  547.1 0.2 reshape.71
  547.3 0.3 fusion.17
  547.6 0.3 broadcast_in_dim.6
  547.9 16.2 %all_to_all.27 = f32[4,1,37248]{2,1,0:T(1,128)S(1)} all-to-all(f32[4,1,37248]{2,1,0:T(1,128)S(1)} %broadcast_in_dim.6), channel_id=1, replica_groups=mesh['fsdp'=64,'tp'=4] {'tp'}, dimensions={0} | all-to-all | bytes 1191936 | tf_op jit(solution)/shard_map/all_to_all | solution.py:14
  564.1 0.6 reduce_sum.46
  564.7 0.9 convert_element_type.30
  565.7 0.2 reshape.74
  565.9 0.1 multiply_convert_fusion
  566.0 0.2 fusion.24
  566.2 0.2 fusion.25
  566.5 0.3 convolution_multiply_fusion.1
  566.8 0.1 copy-done.3
  566.9 0.8 convolution_multiply_fusion
  567.8 0.6 all_to_all.20
  568.3 21.0 %all_to_all.28 = f32[64,1,1568]{2,1,0:T(1,128)S(1)} all-to-all(f32[64,1,1568]{2,1,0:T(1,128)S(1)} %all_to_all.20), channel_id=1, replica_groups=mesh['fsdp'=64,'tp'=4] {'fsdp'}, dimensions={0} | all-to-all | bytes 802816 | tf_op jit(solution)/shard_map/all_to_all | solution.py:36
  589.4 0.3 reduce_sum.49
  589.6 0.2 broadcast_in_dim.16
  589.9 20.6 %all_to_all.29 = f32[64,1,1568]{2,1,0:T(1,128)S(1)} all-to-all(f32[64,1,1568]{2,1,0:T(1,128)S(1)} %broadcast_in_dim.16), channel_id=1, replica_groups=mesh['fsdp'=64,'tp'=4] {'fsdp'}, dimensions={0} | all-to-all | bytes 802816 | tf_op jit(solution)/shard_map/all_to_all | solution.py:14
  610.5 1.0 reduce.3
  611.5 0.3 slice.43
  611.8 0.0 reduce-scatter.2.cloned.1.call-done
  611.8 3.9 fusion.12
  615.7 0.6 broadcast_in_dim.7
  616.3 6.3 all-to-all-start.1
  622.6 0.6 fusion.37
  623.2 0.3 reshape.78
  623.6 0.8 reshape.79
  624.4 0.7 reshape.80
  625.0 2.2 all-to-all-done.1
  627.3 2.0 fusion.15
  629.3 1.9 copy.60
  (28 shorter events, 0.3 us)
Async XLA Ops:
  7.2 511.7 %copy-start = (bf16[384,1536]{1,0:T(8,128)(2,1)S(1)}, bf16[384,1536]{1,0:T(8,128)(2,1)}, u32[]{:S(2)}) copy-start(bf16[384,1536]{1,0:T(8,128)(2,1)} %param.21) | copy-start | bytes 3538948
  7.2 511.6 %all-gather.2.cloned.1.call-start = ((), (), s32[]{:S(2)}) async-start(), calls=%async_computation.5 | async-start | bytes 23429120 | tf_op jit(solution)/shard_map/all_gather | solution.py:75
  9.1 522.2 %copy-start.2 = (bf16[384,256]{1,0:T(8,128)(2,1)S(1)}, bf16[384,256]{1,0:T(8,128)(2,1)}, u32[]{:S(2)}) copy-start(bf16[384,256]{1,0:T(8,128)(2,1)} %param.22) | copy-start | bytes 589828
  9.1 602.7 %reduce-scatter.2.cloned.1.call-start = ((), (), s32[]{:S(2)}) async-start(), calls=%async_computation.6 | async-start | bytes 5406720 | tf_op jit(solution)/shard_map/reduce_scatter | solution.py:166
  531.4 3.6 copy-start.1
  540.5 2.2 copy-start.5
  540.5 2.4 copy-start.6
  540.6 2.6 copy-start.4
  565.9 1.0 copy-start.3
  616.3 10.9 %all-to-all-start.1 = ((f32[4,1,384]{2,1,0:T(1,128)}), f32[4,1,384]{2,1,0:T(1,128)S(1)}, u32[]{:S(2)}, u32[]{:S(2)}) async-start(f32[4,1,384]{2,1,0:T(1,128)} %broadcast_in_dim.7), calls=%async_computation.2 | async-start | bytes 12288 | tf_op jit(solution)/shard_map/all_to_all | solution.py:14
Sparse Core Ops, SparseCore 0:
  10.4 508.4 all-gather.1
  540.7 61.6 reduce-scatter.1
where the time goes:
time: 639 us; the launch traced here: 638 us
  waiting for transfers between devices  512 us (80%)
  blocking collectives  57.8 us (9%)
  matrix products  29.8 us (5%)
  between operations  14.4 us (2%)
  local copies, waits for them, and re-layouts  11.5 us (2%)
  starting transfers between devices  6.42 us (1%)
    all_gather x1, waiting for transfers between devices, in_one_piece(): whole = lax.all_gather(both, axis, axis=dim, tiled=True)  510 us
    all_to_all x2, blocking collectives, from_everyone(): return lax.all_to_all(copies, axis, split_axis=0, concat_axis=0, tiled=True)  36.8 us
    dot_general x3, matrix products, transposed_product(): lax.dot_general(cotangent, piece, (((1,), (1,)), ((), ())), preferred_ele...  21.6 us
    all_to_all x1, blocking collectives, sum_at_owner(): lax.all_to_all(in_blocks(array, dim, count), axis, 0, 0, tiled=True)  21 us
  transfers between devices with their start and end apart: 3, of which 2 were waited for; matrix products, arithmetic and copies ran while one was open for 2% of the time, Pallas kernels for 0%

commit v1 on v0

--- a/solution.py
+++ b/solution.py
@@ -1,12 +1,303 @@
+import functools
+import heapq
 import math
 
 import jax
 import jax.numpy as jnp
 from jax import lax
+from jax.experimental import pallas as pl
+from jax.experimental.pallas import tpu as pltpu
 from jax.sharding import PartitionSpec as P
 
 norm_eps = 1e-05
 adapter_scale = 2.0
+
+MESH = pl.DeviceIdType.MESH
+NY, NZ = 4, 8
+SLOT = 48
+CHUNKS = (8, 8, 8, 8, 8, 8, 8, 4, 4)
+
+
+def forwards(have, item):
+    part, dy, dz, half = item
+    out = []
+    if part == 0:
+        if dz == 0:
+            if dy == 0:
+                out += [("y+", (0, 1, 0, None)), ("y-", (0, -1, 0, None))]
+            elif dy == 1:
+                out += [("y+", (0, 2, 0, 0))]
+            elif dy == -1:
+                out += [("y-", (0, 2, 0, 1))]
+            if half is None or (0, 2, 0, 1 - half) in have:
+                out += [("z+", (0, dy, 1, None)), ("z-", (0, dy, -1, None))]
+        elif dz > 0:
+            if dz < 3 or (dz == 3 and dy in (0, 1)):
+                out += [("z+", (0, dy, dz + 1, None))]
+        elif dz > -3:
+            out += [("z-", (0, dy, dz - 1, None))]
+        elif dy in (-1, 2):
+            out += [("z-", (0, dy, 4, None))]
+    elif dy == 0:
+        if dz == 0:
+            out += [("z+", (1, 0, 1, None)), ("z-", (1, 0, -1, None))]
+        elif 0 < dz < 4:
+            out += [("z+", (1, 0, dz + 1, 0 if dz == 3 else None))]
+        elif dz < 0:
+            out += [("z-", (1, 0, 4 if dz == -3 else dz - 1, 1 if dz == -3 else None))]
+        if half is None or (1, 0, 4, 1 - half) in have:
+            out += [("y+", (1, 1, dz, None)), ("y-", (1, -1, dz, None))]
+    elif dy == 1 and dz in (0, 1, 2, 3):
+        out += [("y+", (1, 2, dz, None))]
+    elif dy == -1 and dz in (-1, -2, -3, 4):
+        out += [("y-", (1, 2, dz, None))]
+    return out
+
+
+def gather_plan(rows, rate=44.0, latency=1.9):
+    size = [r * 4.096 for r in rows]
+    free = dict.fromkeys(("y+", "y-", "z+", "z-"), 0.0)
+    have, events, log = set(), [], []
+
+    def issue(now, link, item):
+        span = size[item[0]] * (1.0 if item[3] is None else 0.5) / rate
+        free[link] = max(now, free[link]) + span
+        heapq.heappush(events, (free[link] + latency, len(log) + len(events), link, item))
+
+    first = []
+    for item in ((0, 0, 0, None), (1, 0, 0, None)):
+        have.add(item)
+        first += forwards(have, item)
+    first = [e for e in first if e[0][0] == "y"] + [e for e in reversed(first) if e[0][0] == "z"]
+    for link, item in first:
+        issue(0.0, link, item)
+    count = len(first)
+    while events:
+        now, _, link, item = heapq.heappop(events)
+        have.add(item)
+        onward = forwards(have, item)
+        log.append((now, item, onward))
+        for link, new in onward:
+            issue(now + 0.1, link, new)
+    slots = {(0, 0, 0): 0, (1, 0, 0): 1}
+    whole = []
+    for index, (now, item, _) in enumerate(log):
+        key = item[:3]
+        if item[3] is None or (*key, 1 - item[3]) in [e[1] for e in log[:index]]:
+            slots[key] = len(slots)
+            whole.append(index)
+    return first, [(item, onward) for _, item, onward in log], slots
+
+
+def gather_multiply_kernel(
+    rows, wq, wk, wv, gq, gk, gv, out, wbuf, gbuf, keep, csend, crecv, xs, xr,
+    load_sem, wsend_sem, wrecv_sem, g_sem, csend_sem, crecv_sem, xsend_sem, xrecv_sem,
+):
+    f = lax.axis_index("fsdp")
+    t = lax.axis_index("tp")
+    y, z, x_lo = f // 16, (f // 2) % 8, f % 2
+    x_hi, core = t // 2, t % 2
+    tokens = gq.shape[0]
+    first, log, slots = gather_plan(rows)
+    where = {v: k for k, v in slots.items()}
+
+    def place(yy, zz, xx):
+        return (yy % NY) * 16 + (zz % NZ) * 2 + xx
+
+    link_device = {
+        "y+": (place(y + 1, z, x_lo), t),
+        "y-": (place(y + NY - 1, z, x_lo), t),
+        "z+": (place(y, z + 1, x_lo), t),
+        "z-": (place(y, z + NZ - 1, x_lo), t),
+    }
+    mate = (place(y, z, 1 - x_lo), t)
+    twin = (f, x_hi * 2 + 1 - core)
+
+    loads = []
+    own_half = (x_lo + core) % 2
+    own_rows = pl.ds(pl.multiple_of(own_half * tokens, 128), tokens)
+    column = 0
+    for index, (w, g) in enumerate(((wq, gq), (wk, gk), (wv, gv))):
+        width = w.shape[1]
+        columns = pl.ds(column, width)
+        loads.append(pltpu.make_async_copy(w.at[pl.ds(0, rows[0])], wbuf.at[0, pl.ds(0, rows[0]), columns], load_sem.at[3 * index]))
+        loads.append(pltpu.make_async_copy(w.at[pl.ds(rows[0], rows[1])], wbuf.at[1, pl.ds(0, rows[1]), columns], load_sem.at[3 * index + 1]))
+        loads.append(pltpu.make_async_copy(g, gbuf.at[own_rows, columns], load_sem.at[3 * index + 2]))
+        column += width
+    for load in loads:
+        load.start()
+
+    barrier = pltpu.get_barrier_semaphore()
+    partners = list(link_device.values())
+    for dhi in (0, 1):
+        for dlo in (0, 1):
+            for dc in (0, 1):
+                if dhi or dlo or dc:
+                    partners.append((place(y, z, (x_lo + dlo) % 2), ((x_hi + dhi) % 2) * 2 + (core + dc) % 2))
+    for device in partners:
+        pl.semaphore_signal(barrier, inc=1, device_id=device, device_id_type=MESH)
+    pl.semaphore_wait(barrier, len(partners))
+    for load in loads:
+        load.wait()
+
+    g_copy = pltpu.make_async_remote_copy(
+        src_ref=gbuf.at[own_rows], dst_ref=gbuf.at[own_rows], send_sem=g_sem.at[0], recv_sem=g_sem.at[1],
+        device_id=mate, device_id_type=MESH,
+    )
+
+    event_index = {item: index for index, (item, _) in enumerate(log)}
+    half_width = wbuf.shape[2] // 2
+    sends = []
+
+    def block(item):
+        part, dy, dz, half = item
+        ref = wbuf.at[slots[(part, dy, dz)], pl.ds(0, rows[part])]
+        if half is not None:
+            ref = wbuf.at[slots[(part, dy, dz)], pl.ds(0, rows[part]), pl.ds(half * half_width, half_width)]
+        return ref
+
+    def source(item, have):
+        return item
+
+    def send(origin, link, item):
+        part, dy, dz, half = item
+        src = wbuf.at[slots[origin[:3]], pl.ds(0, rows[part])]
+        if half is not None:
+            src = wbuf.at[slots[origin[:3]], pl.ds(0, rows[part]), pl.ds(half * half_width, half_width)]
+        index = event_index[item]
+        copy = pltpu.make_async_remote_copy(
+            src_ref=src, dst_ref=block(item), send_sem=wsend_sem.at[index], recv_sem=wrecv_sem.at[index],
+            device_id=link_device[link], device_id_type=MESH,
+        )
+        copy.start()
+        sends.append(copy)
+
+    for link, item in first:
+        send((item[0], 0, 0, None), link, item)
+    g_copy.start()
+
+    starts = [sum(CHUNKS[:k]) for k in range(len(CHUNKS))]
+    core_copies = {}
+    same = x_lo == core
+    my_chip = x_hi * 2 + x_lo
+
+    def multiply(k):
+        begin, count = starts[k], CHUNKS[k]
+        lines = wbuf[begin : begin + count].reshape(count * SLOT, wbuf.shape[2])
+        product = lax.dot_general(lines, gbuf[...], (((1,), (1,)), ((), ())), preferred_element_type=jnp.float32)
+        keep[begin * SLOT : (begin + count) * SLOT, :] = product[:, :tokens]
+        csend[begin : begin + count] = product[:, tokens:].astype(jnp.bfloat16).reshape(count, SLOT, tokens)
+        copy = pltpu.make_async_remote_copy(
+            src_ref=csend.at[pl.ds(begin, count)], dst_ref=crecv.at[pl.ds(begin, count)],
+            send_sem=csend_sem.at[k], recv_sem=crecv_sem.at[k], device_id=twin, device_id_type=MESH,
+        )
+        copy.start()
+        core_copies[k] = copy
+
+    def pass_on(k):
+        begin, count = starts[k], CHUNKS[k]
+        core_copies[k].wait_recv()
+        total = keep[begin * SLOT : (begin + count) * SLOT, :] + crecv[begin : begin + count].reshape(count * SLOT, tokens).astype(jnp.float32)
+        xs[begin : begin + count] = total.astype(jnp.bfloat16).reshape(count, SLOT, tokens)
+        for slot in range(begin, begin + count):
+            part, dy, dz = where[slot]
+            owner_y, owner_z = (y + NY - dy) % NY, (z + NZ - dz) % NZ
+            src = xs.at[slot, pl.ds(0, rows[part])]
+            dst = xr.at[my_chip, owner_z, pl.ds(part * rows[0], rows[part])]
+            own = jnp.logical_and(same, owner_y == t)
+
+            @pl.when(own)
+            def _():
+                pltpu.make_async_copy(src, dst, xrecv_sem.at[my_chip]).start()
+
+            @pl.when(jnp.logical_not(own))
+            def _():
+                pltpu.make_async_remote_copy(
+                    src_ref=src, dst_ref=dst, send_sem=xsend_sem, recv_sem=xrecv_sem.at[my_chip],
+                    device_id=(place(y, z, core), owner_y), device_id_type=MESH,
+                ).start()
+
+    done_slots, done_chunks, passed = 2, 0, 0
+    have = {(0, 0, 0, None), (1, 0, 0, None)}
+    g_waited = False
+    for index, (item, onward) in enumerate(log):
+        pltpu.make_async_copy(block(item), block(item), wrecv_sem.at[index]).wait()
+        have.add(item)
+        for link, new in onward:
+            send(item, link, new)
+        if item[3] is None or (*item[:3], 1 - item[3]) in have:
+            done_slots += 1
+        if done_chunks >= 1 and passed < done_chunks and (index % 2 == 0):
+            pass
+        while done_chunks < len(CHUNKS) and starts[done_chunks] + CHUNKS[done_chunks] <= done_slots and index >= 31:
+            if not g_waited:
+                g_copy.wait_recv()
+                g_waited = True
+            multiply(done_chunks)
+            done_chunks += 1
+            if done_chunks - passed > 1:
+                pass_on(passed)
+                passed += 1
+            if index < len(log) - 1:
+                break
+    while passed < len(CHUNKS):
+        pass_on(passed)
+        passed += 1
+    for chip in range(4):
+        pltpu.make_async_copy(xr.at[chip], xr.at[chip], xrecv_sem.at[chip]).wait()
+    for half in range(2):
+        out[:, half] = xr[half].astype(jnp.float32) + xr[2 + half].astype(jnp.float32)
+
+    g_copy.wait_send()
+    for copy in sends:
+        copy.wait_send()
+    for copy in core_copies.values():
+        copy.wait_send()
+
+    @pl.when(same)
+    def _():
+        pltpu.make_async_copy(xr.at[pl.ds(0, 3)], xr.at[pl.ds(0, 3)], xsend_sem).wait()
+
+    @pl.when(jnp.logical_not(same))
+    def _():
+        pltpu.make_async_copy(xr, xr, xsend_sem).wait()
+
+
+def gather_multiply(weights, cotangents):
+    tokens = cotangents[0].shape[0]
+    owned = weights[0].shape[0]
+    rows = (40, owned - 40)
+    width = sum(w.shape[1] for w in weights)
+    events = len(gather_plan(rows)[1])
+    slots = 2 * NY * NZ
+    chunks = len(CHUNKS)
+    bf16 = jnp.bfloat16
+    return pl.pallas_call(
+        functools.partial(gather_multiply_kernel, rows),
+        out_shape=jax.ShapeDtypeStruct((NZ, 2, owned, tokens), jnp.float32),
+        in_specs=[pl.BlockSpec(memory_space=pl.ANY)] * 6,
+        out_specs=pl.BlockSpec(memory_space=pltpu.VMEM),
+        scratch_shapes=[
+            pltpu.VMEM((slots, SLOT, width), bf16),
+            pltpu.VMEM((2 * tokens, width), bf16),
+            pltpu.VMEM((slots * SLOT, tokens), jnp.float32),
+            pltpu.VMEM((slots, SLOT, tokens), bf16),
+            pltpu.VMEM((slots, SLOT, tokens), bf16),
+            pltpu.VMEM((slots, SLOT, tokens), bf16),
+            pltpu.VMEM((4, NZ, owned, tokens), bf16),
+            pltpu.SemaphoreType.DMA((9,)),
+            pltpu.SemaphoreType.DMA((events,)),
+            pltpu.SemaphoreType.DMA((events,)),
+            pltpu.SemaphoreType.DMA((2,)),
+            pltpu.SemaphoreType.DMA((chunks,)),
+            pltpu.SemaphoreType.DMA((chunks,)),
+            pltpu.SemaphoreType.DMA,
+            pltpu.SemaphoreType.DMA((4,)),
+        ],
+        compiler_params=pltpu.CompilerParams(collective_id=0, has_side_effects=True, vmem_limit_bytes=52 << 20),
+        cost_estimate=pl.CostEstimate(flops=9 * 10**9, bytes_accessed=6 * 10**6, transcendentals=0),
+        name="gather_multiply",
+    )(*weights, *cotangents)
 
 
 def from_everyone(array, axis):
@@ -18,68 +309,12 @@
     return from_everyone(array, axis).sum(axis=0)
 
 
-def in_one(arrays, axis):
+def in_one(arrays, axis, total_of):
     ends = [0]
     for a in arrays:
         ends.append(ends[-1] + a.size)
-    total = over_copies(jnp.concatenate([a.ravel() for a in arrays]), axis)
+    total = total_of(jnp.concatenate([a.ravel() for a in arrays]), axis)
     return tuple((total[b:e].reshape(a.shape) for a, b, e in zip(arrays, ends, ends[1:])))
-
-
-def in_blocks(array, dim, count):
-    before, after = (array.shape[:dim], array.shape[dim + 1 :])
-    return jnp.moveaxis(array.reshape(*before, count, -1, *after), dim, 0)
-
-
-def sum_at_owner(array, axis, dim):
-    count = lax.axis_size(axis)
-    pieces = lax.all_to_all(in_blocks(array, dim, count), axis, 0, 0, tiled=True)
-    return jnp.sum(pieces, axis=0)
-
-
-def filled_up(lines, count):
-    spare = -lines.shape[0] % count
-    if not spare:
-        return lines
-    return jnp.concatenate([lines, jnp.zeros((spare, *lines.shape[1:]), lines.dtype)])
-
-
-def joined_along(pieces, dim):
-    lengths = list(pieces.shape[1:])
-    lengths[dim] *= pieces.shape[0]
-    return jnp.moveaxis(pieces, 0, dim).reshape(lengths)
-
-
-def gathered_copies(array, axis, dim):
-    return joined_along(from_everyone(array, axis), dim)
-
-
-def sum_by_parts(array, axes):
-    own = sum_at_owner(filled_up(array, lax.axis_size(axes)), axes, 0)
-    whole = gathered_copies(own, axes, 0)
-    return whole[: len(array)].reshape(array.shape)
-
-
-def packed_total(arrays, axis):
-    line, at, done = (jnp.concatenate([a.reshape(-1) for a in arrays]), 0, [])
-    total = sum_by_parts(line, axis)
-    for a in arrays:
-        done.append(total[at : at + a.size].reshape(a.shape))
-        at += a.size
-    return tuple(done)
-
-
-def in_one_piece(arrays, axis, dim, along):
-    widths = [a.shape[along] for a in arrays]
-    both = jnp.concatenate(arrays, axis=along)
-    whole = lax.all_gather(both, axis, axis=dim, tiled=True)
-    return tuple(jnp.split(whole, [sum(widths[:k]) for k in range(1, len(widths))], axis=along))
-
-
-def transposed_product(cotangent, piece):
-    return lax.dot_general(
-        cotangent, piece, (((1,), (1,)), ((), ())), preferred_element_type=jnp.float32
-    )
 
 
 def shards(
@@ -130,6 +365,7 @@
             adapter_output_slice,
         ),
         "tp",
+        over_copies,
     )
     inverse_root_mean = lax.rsqrt(squared_total / full_width + norm_eps)[:, None]
     adapter_input = adapter_input_unnormed * inverse_root_mean[None]
@@ -152,20 +388,13 @@
             for slice_member in range(3)
         )
     )
-    grad_down, grad_up_query, grad_up_key, grad_up_value = packed_total(
-        (down_local, up_local[0], up_local[1], up_local[2]), "fsdp"
-    )
-    pieces = in_one_piece(
-        (query_projection_weight, key_projection_weight, value_projection_weight), "fsdp", 0, 1
-    )
-    block = (
-        transposed_product(query_cotangent, pieces[0])
-        + transposed_product(key_cotangent, pieces[1])
-        + transposed_product(value_cotangent, pieces[2])
-    )
-    backward_result = lax.psum_scatter(
-        block.astype(jnp.bfloat16), "tp", scatter_dimension=1, tiled=True
-    ).astype(jnp.float32)
+    grad_down, grad_up_query, grad_up_key, grad_up_value = in_one(
+        (down_local, up_local[0], up_local[1], up_local[2]), "fsdp", lax.psum
+    )
+    back_t = gather_multiply(
+        (query_projection_weight, key_projection_weight, value_projection_weight), cotangent_list
+    )
+    backward_result = back_t.reshape(owned_width, number_of_rows).T
     backward_result = backward_result + adapter_scale * jnp.einsum(
         "ktr,krd->td", output_lowrank, down_owned_slice, preferred_element_type=jnp.float32
     )

time: 639 us -> 735 us (1.15)
  the two profiles are of different devices: /device:TPU:1 before, /device:TPU:4 now
where the time goes in v1:
time: 735 us
  waiting for transfers between devices  585 us (80%)
  Pallas kernels  88.2 us (12%)
  local copies, waits for them, and re-layouts  18.8 us (3%)
  between operations  14.2 us (2%)
  starting transfers between devices  11.1 us (2%)
  matrix products  9.26 us (1%)
  other arithmetic  8.51 us (1%)
    psum x1, waiting for transfers between devices, in_one(): total = total_of(jnp.concatenate([a.ravel() for a in arrays]), axis)  584 us
    pallas_call x1, Pallas kernels, gather_multiply(): pl.pallas_call(functools.partial(gather_multiply_kernel, rows), out_shape...  88.2 us
  transfers between devices with their start and end apart: 3, of which 2 were waited for; matrix products, arithmetic and copies ran while one was open for 1% of the time, Pallas kernels for 12%

profile of v1, /device:TPU:4, one launch (start us, length us, event | category | flops | bytes accessed | tf_op | source)
XLA Modules:
  0.0 734.8 jit_solution(11200616869812254168)
XLA Ops:
  7.2 0.0 copy-start
  7.2 1.2 convolution_bitcast_fusion.1
  8.4 1.1 convolution_bitcast_fusion.2
  9.5 1.7 convolution_bitcast_fusion.3
  11.3 0.2 copy.29
  11.5 0.8 reshape.75
  12.4 0.0 copy-done.7
  12.4 0.9 fusion.11
  13.2 0.8 dynamic_slice.7
  14.0 0.6 copy-done.9
  14.6 0.0 copy-done
  14.6 0.0 copy-start.4
  14.6 0.0 copy-start.5
  14.6 0.0 copy-start.6
  14.7 2.0 fusion.15
  16.6 1.9 copy.28
  18.6 1.9 reshape.74
  20.4 0.9 pad_maximum_fusion.1
  21.4 1.1 broadcast_in_dim.4
  22.5 6.3 all-to-all-start
  28.9 88.2 %gather_multiply.1 = f32[8,2,88,384]{3,2,1,0:T(8,128)} custom-call(bf16[88,1536]{1,0:T(8,128)(2,1)S(1)} %copy-done.4, bf16[88,256]{1,0:T(8,128)(2,1)S(1)} %copy-done.5, bf16[88,256]{1,0:T(8,128)(2,1)S(1)} %copy-done.6, bf16[384,1536]{1,0:T(8,128)(2,1)S(1)} %copy-done.1, bf16[384,256]{1,0:T(8,128)(2,1)S(1)} %copy-done.3, bf16[384,256]{1,0:T(8,128)(2,1)S(1)} %copy-done.2), custom_call_target="tpu_custom_call" | custom-call | flops 8999999488 | bytes 6000000 | tf_op jit(solution)/shard_map/gather_multiply/pallas_call | solution.py:275
  117.1 3.0 copy.31
  120.1 0.0 all-to-all-done
  120.1 1.6 reduce_sum.37
  121.7 0.0 copy-start.10
  121.8 1.0 reshape.78
  122.8 1.2 multiply_convert_fusion
  124.0 0.2 fusion.18
  124.2 0.2 fusion.19
  124.3 0.3 convolution_multiply_fusion.1
  124.7 0.2 convert_element_type.18
  124.9 0.5 convolution_multiply_fusion
  125.4 1.1 copy-done.8
  126.5 2.1 fusion.6
  128.6 0.6 broadcast_in_dim.5
  129.2 4.8 all-to-all-start.1
  134.1 0.8 pad_maximum_fusion
  134.9 0.0 all-reduce.2.cloned.1.call-update
  134.9 0.9 all-to-all-done.1
  135.9 3.0 fusion.9
  138.9 583.8 %all-reduce.2.cloned.1.call-done = f32[100352]{0:T(1024)} async-done(((f32[100352]{0:T(1024)}), f32[100352]{0:T(1024)}) %all-reduce.2.cloned.1.call-update) | async-done | bytes 401424 | tf_op jit(solution)/shard_map/psum | solution.py:316
  722.7 1.0 slice.69
  723.6 0.8 reshape.82
  724.4 0.9 slice.70
  725.3 0.7 reshape.83
  726.0 0.7 fusion.31
  726.7 0.6 slice.60
  727.3 0.6 slice.62
  (24 shorter events, 0.2 us)
Async XLA Ops:
  7.2 7.4 %copy-start = (bf16[3,16,5632]{2,1,0:T(8,128)(2,1)S(1)}, bf16[3,16,5632]{2,1,0:T(8,128)(2,1)}, u32[]{:S(2)}) copy-start(bf16[3,16,5632]{2,1,0:T(8,128)(2,1)} %param.17) | copy-start | bytes 1622020
  7.2 5.2 copy-start.7
  14.0 0.6 copy-start.9
  14.6 14.2 %copy-start.1 = (bf16[384,1536]{1,0:T(8,128)(2,1)S(1)}, bf16[384,1536]{1,0:T(8,128)(2,1)}, u32[]{:S(2)}) copy-start(bf16[384,1536]{1,0:T(8,128)(2,1)} %gq.1) | copy-start | bytes 3538948
  14.6 14.2 %copy-start.2 = (bf16[384,256]{1,0:T(8,128)(2,1)S(1)}, bf16[384,256]{1,0:T(8,128)(2,1)}, u32[]{:S(2)}) copy-start(bf16[384,256]{1,0:T(8,128)(2,1)} %gv.1) | copy-start | bytes 589828
  14.6 14.2 %copy-start.3 = (bf16[384,256]{1,0:T(8,128)(2,1)S(1)}, bf16[384,256]{1,0:T(8,128)(2,1)}, u32[]{:S(2)}) copy-start(bf16[384,256]{1,0:T(8,128)(2,1)} %gk.1) | copy-start | bytes 589828
  14.6 14.2 %copy-start.4 = (bf16[88,1536]{1,0:T(8,128)(2,1)S(1)}, bf16[88,1536]{1,0:T(8,128)(2,1)}, u32[]{:S(2)}) copy-start(bf16[88,1536]{1,0:T(8,128)(2,1)} %wq.1) | copy-start | bytes 811012
  14.6 14.2 %copy-start.5 = (bf16[88,256]{1,0:T(8,128)(2,1)S(1)}, bf16[88,256]{1,0:T(8,128)(2,1)}, u32[]{:S(2)}) copy-start(bf16[88,256]{1,0:T(8,128)(2,1)} %wk.1) | copy-start | bytes 135172
  14.6 14.2 %copy-start.6 = (bf16[88,256]{1,0:T(8,128)(2,1)S(1)}, bf16[88,256]{1,0:T(8,128)(2,1)}, u32[]{:S(2)}) copy-start(bf16[88,256]{1,0:T(8,128)(2,1)} %wv.1) | copy-start | bytes 135172
  22.5 97.6 %all-to-all-start = ((f32[4,1,37248]{2,1,0:T(1,128)}), f32[4,1,37248]{2,1,0:T(1,128)}, u32[]{:S(2)}, u32[]{:S(2)}) async-start(f32[4,1,37248]{2,1,0:T(1,128)} %broadcast_in_dim.4), calls=%async_computation | async-start | bytes 1191936 | tf_op jit(solution)/shard_map/all_to_all | solution.py:305
  121.7 3.2 copy-start.10
  124.9 1.6 copy-start.8
  129.2 6.6 all-to-all-start.1
  134.0 588.6 %all-reduce.2.cloned.1.call-start = ((), (), s32[]{:S(2)}) async-start(), calls=%async_computation.2 | async-start | bytes 802816 | tf_op jit(solution)/shard_map/psum | solution.py:316
Sparse Core Ops, SparseCore 0:
  137.5 585.1 all-reduce.1

commit v2 on v1

v2 whole, which is shorter than its diff:
```python
import functools
import heapq
import math

import jax
import jax.numpy as jnp
from jax import lax
from jax.experimental import pallas as pl
from jax.experimental.pallas import tpu as pltpu
from jax.sharding import PartitionSpec as P

norm_eps = 1e-05
adapter_scale = 2.0

MESH = pl.DeviceIdType.MESH
NY, NZ = 4, 8
SLOT = 48
CHUNKS = (8, 8, 8, 8, 8, 8, 8, 4, 4)
G_PIECES = 4
G_EVENT = 33


def forwards(have, item):
    part, dy, dz, half = item
    out = []
    if part == 0:
        if dz == 0:
            if dy == 0:
                out += [("y+", (0, 1, 0, None)), ("y-", (0, -1, 0, None))]
            elif dy == 1:
                out += [("y+", (0, 2, 0, 0))]
            elif dy == -1:
                out += [("y-", (0, 2, 0, 1))]
            if half is None or (0, 2, 0, 1 - half) in have:
                out += [("z+", (0, dy, 1, None)), ("z-", (0, dy, -1, None))]
        elif dz > 0:
            if dz < 3 or (dz == 3 and dy in (0, 1)):
                out += [("z+", (0, dy, dz + 1, None))]
        elif dz > -3:
            out += [("z-", (0, dy, dz - 1, None))]
        elif dy in (-1, 2):
            out += [("z-", (0, dy, 4, None))]
    elif dy == 0:
        if dz == 0:
            out += [("z+", (1, 0, 1, None)), ("z-", (1, 0, -1, None))]
        elif 0 < dz < 4:
            out += [("z+", (1, 0, dz + 1, 0 if dz == 3 else None))]
        elif dz < 0:
            out += [("z-", (1, 0, 4 if dz == -3 else dz - 1, 1 if dz == -3 else None))]
        if half is None or (1, 0, 4, 1 - half) in have:
            out += [("y+", (1, 1, dz, None)), ("y-", (1, -1, dz, None))]
    elif dy == 1 and dz in (0, 1, 2, 3):
        out += [("y+", (1, 2, dz, None))]
    elif dy == -1 and dz in (-1, -2, -3, 4):
        out += [("y-", (1, 2, dz, None))]
    return out


def gather_plan(rows, rate=44.0, latency=1.9):
    size = [r * 4.096 for r in rows]
    free = dict.fromkeys(("y+", "y-", "z+", "z-"), 0.0)
    have, events, log = set(), [], []

    def issue(now, link, item):
        span = size[item[0]] * (1.0 if item[3] is None else 0.5) / rate
        free[link] = max(now, free[link]) + span
        heapq.heappush(events, (free[link] + latency, len(log) + len(events), link, item))

    first = []
    for item in ((0, 0, 0, None), (1, 0, 0, None)):
        have.add(item)
        first += forwards(have, item)
    first = [e for e in first if e[0][0] == "y"] + [e for e in reversed(first) if e[0][0] == "z"]
    for link, item in first:
        issue(0.0, link, item)
    count = len(first)
    while events:
        now, _, link, item = heapq.heappop(events)
        have.add(item)
        onward = forwards(have, item)
        log.append((now, item, onward))
        for link, new in onward:
            issue(now + 0.1, link, new)
    slots = {(0, 0, 0): 0, (1, 0, 0): 1}
    whole = []
    for index, (now, item, _) in enumerate(log):
        key = item[:3]
        if item[3] is None or (*key, 1 - item[3]) in [e[1] for e in log[:index]]:
            slots[key] = len(slots)
            whole.append(index)
    return first, [(item, onward) for _, item, onward in log], slots


def dot_nt(a, b):
    return lax.dot_general(a, b, (((1,), (1,)), ((), ())), preferred_element_type=jnp.float32)


def as_column(row):
    return jnp.transpose(jnp.broadcast_to(row, (128, row.shape[1])))[:, :1]


def layer_kernel(
    rows, wq, wk, wv, gq, gk, gv, tokens_hbm, gain_all, down_all, uq, uk, uv,
    grad, down_out, upq_out, upk_out, upv_out,
    wbuf, gbuf, keep, csend, crecv, xs, xr,
    tok, tok_t, acc, turned, gain_column, low, low_total, out_low_buf, inverse, inner_buf,
    arw, ar1, ar2, ar3, arg,
    load_sem, wsend_sem, wrecv_sem, gsend_sem, grecv_sem, csend_sem, crecv_sem, xsend_sem, xrecv_sem,
    lsend_sem, lrecv_sem, asend_sem, arecv_sem, isend_sem, irecv_sem,
):
    f = lax.axis_index("fsdp")
    t = lax.axis_index("tp")
    y, z, x_lo = f // 16, (f // 2) % 8, f % 2
    x_hi, core = t // 2, t % 2
    tokens, owned_width = tokens_hbm.shape
    full_width = gain_all.shape[1]
    f32, bf16 = jnp.float32, jnp.bfloat16
    first, log, slots = gather_plan(rows)
    where = {v: k for k, v in slots.items()}

    def place(yy, zz, xx):
        return (yy % NY) * 16 + (zz % NZ) * 2 + xx

    link_device = {
        "y+": (place(y + 1, z, x_lo), t),
        "y-": (place(y + NY - 1, z, x_lo), t),
        "z+": (place(y, z + 1, x_lo), t),
        "z-": (place(y, z + NZ - 1, x_lo), t),
    }
    mate = (place(y, z, 1 - x_lo), t)
    twin = (f, x_hi * 2 + 1 - core)
    across = (f, (1 - x_hi) * 2 + core)

    def remote(src, dst, send_sem, recv_sem, device):
        return pltpu.make_async_remote_copy(
            src_ref=src, dst_ref=dst, send_sem=send_sem, recv_sem=recv_sem, device_id=device, device_id_type=MESH
        )

    def landed(ref, sem):
        pltpu.make_async_copy(ref, ref, sem).wait()

    started = []

    def send_now(*args):
        copy = remote(*args)
        copy.start()
        started.append(copy)
        return copy

    loads, token_load = [], pltpu.make_async_copy(tokens_hbm, tok, load_sem.at[9])
    own_half = (x_lo + core) % 2
    own_begin = pl.multiple_of(own_half * tokens, 128)
    column, spans = 0, []
    for index, (w, g) in enumerate(((wq, gq), (wk, gk), (wv, gv))):
        width = w.shape[1]
        columns = pl.ds(column, width)
        spans.append((column, width))
        loads.append(pltpu.make_async_copy(w.at[pl.ds(0, rows[0])], wbuf.at[0, pl.ds(0, rows[0]), columns], load_sem.at[3 * index]))
        loads.append(pltpu.make_async_copy(w.at[pl.ds(rows[0], rows[1])], wbuf.at[1, pl.ds(0, rows[1]), columns], load_sem.at[3 * index + 1]))
        column += width
    for index, g in enumerate((gq, gk, gv)):
        columns = pl.ds(*spans[index])
        loads.append(pltpu.make_async_copy(g, gbuf.at[pl.ds(own_begin, tokens), columns], load_sem.at[3 * index + 2]))
    for load in loads:
        load.start()
    token_load.start()

    barrier = pltpu.get_barrier_semaphore()
    partners = [(place(y + k, z, x_lo), t) for k in range(1, NY)] + [(place(y, z + k, x_lo), t) for k in range(1, NZ)]
    for dhi in (0, 1):
        for dlo in (0, 1):
            for dc in (0, 1):
                if dhi or dlo or dc:
                    partners.append((place(y, z, (x_lo + dlo) % 2), ((x_hi + dhi) % 2) * 2 + (core + dc) % 2))
    for device in partners:
        pl.semaphore_signal(barrier, inc=1, device_id=device, device_id_type=MESH)
    pl.semaphore_wait(barrier, len(partners))
    for load in loads:
        load.wait()

    event_index = {item: index for index, (item, _) in enumerate(log)}
    half_width = wbuf.shape[2] // 2

    def block(slot, part, half):
        if half is None:
            return wbuf.at[slot, pl.ds(0, rows[part])]
        return wbuf.at[slot, pl.ds(0, rows[part]), pl.ds(half * half_width, half_width)]

    def forward(origin, link, item):
        part, half, index = item[0], item[3], event_index[item]
        send_now(
            block(slots[origin[:3]], part, half), block(slots[item[:3]], part, half),
            wsend_sem.at[index], wrecv_sem.at[index], link_device[link],
        )

    for link, item in first:
        forward((item[0], 0, 0), link, item)

    g_lines = tokens // G_PIECES

    def g_piece(k):
        return gbuf.at[pl.ds(pl.multiple_of(own_half * tokens + k * g_lines, 32), g_lines)]

    def g_send(k):
        send_now(g_piece(k), g_piece(k), gsend_sem.at[k], grecv_sem.at[k], mate)

    def g_wait():
        for k in range(G_PIECES):
            landed(gbuf.at[pl.ds(0, g_lines)], grecv_sem.at[k])

    gain_row = gain_all[:, pl.ds(pl.multiple_of(t * owned_width, 128), owned_width)]
    down = down_all[:, pl.ds(pl.multiple_of(t * owned_width, 128), owned_width)]
    rank3, rank = down.shape[0], down.shape[0] // 3

    def low_products():
        token_load.wait()
        scaled = down.astype(f32) * gain_row
        high = scaled.astype(bf16)
        rest = scaled - high.astype(f32)
        middle = rest.astype(bf16)
        lowest = (rest - middle.astype(f32)).astype(bf16)
        lines = tok[...]
        for begin, part in ((0, high), (1, middle), (2, lowest)):
            term = dot_nt(part, lines)
            low[0, 0:rank3] = term if begin == 0 else low[0, 0:rank3] + term
        for m, up in enumerate((uq, uk, uv)):
            begin, width = spans[m]
            own = gbuf[pl.ds(own_begin, tokens), begin : begin + width]
            low[0, rank3 + m * rank : rank3 + (m + 1) * rank] = dot_nt(up[...], own)
        squares = lines.astype(f32) * lines.astype(f32)
        high = squares.astype(bf16)
        lowest = (squares - high.astype(f32)).astype(bf16)
        ones = jnp.ones((16, owned_width), bf16)
        low[0, 2 * rank3 : 2 * rank3 + 8] = (dot_nt(ones, high) + dot_nt(ones, lowest))[:8]
        send_now(low.at[0], low.at[1], lsend_sem.at[0], lrecv_sem.at[0], twin)

    def low_pair():
        landed(low.at[1], lrecv_sem.at[0])
        low[2] = low[0] + low[1]
        send_now(low.at[2], low.at[3], lsend_sem.at[1], lrecv_sem.at[1], across)

    gradient_scale = adapter_scale / math.sqrt(tokens * 64)

    def low_all():
        landed(low.at[3], lrecv_sem.at[1])
        low_total[...] = low[2] + low[3]
        inverse_row = lax.rsqrt(low_total[2 * rank3 : 2 * rank3 + 8] / full_width + norm_eps)
        inverse[...] = inverse_row
        in_low = (low_total[0:rank3] * inverse_row[:1]).astype(bf16)
        out_low = low_total[rank3 : 2 * rank3].astype(bf16)
        out_low_buf[...] = out_low
        unit = tok[...].astype(f32) * as_column(inverse_row[:1])
        normed = (unit * gain_row).astype(bf16)
        local = gradient_scale * jnp.dot(out_low, normed, preferred_element_type=f32)
        at = 0
        for j in range(owned_width // 128):
            arw[at : at + rank3] = local[:, j * 128 : (j + 1) * 128]
            at += rank3
        for m in range(3):
            begin, width = spans[m]
            own = gbuf[pl.ds(own_begin, tokens), begin : begin + width]
            local = gradient_scale * jnp.dot(in_low[m * rank : (m + 1) * rank], own, preferred_element_type=f32)
            for j in range(width // 128):
                arw[at : at + rank] = local[:, j * 128 : (j + 1) * 128]
                at += rank
        arw[at:] = jnp.zeros((arw.shape[0] - at, 128), f32)
        send_now(arw.at[pl.ds(pl.multiple_of((1 - x_lo) * 512, 16), 512)], ar1, asend_sem.at[0], arecv_sem.at[0], mate)

    def ar_rows(xx, yy=None, zz=None):
        if yy is None:
            return pl.ds(pl.multiple_of(xx * 512, 16), 512)
        if zz is None:
            return pl.ds(pl.multiple_of(xx * 512 + yy * 128, 16), 128)
        return pl.ds(pl.multiple_of(xx * 512 + yy * 128 + zz * 16, 16), 16)

    def sum_x():
        landed(ar1, arecv_sem.at[0])
        arw[ar_rows(x_lo)] = arw[ar_rows(x_lo)] + ar1[...]
        for k in range(1, NY):
            other = (y + k) % NY
            send_now(arw.at[ar_rows(x_lo, other)], ar2.at[k - 1], asend_sem.at[k], arecv_sem.at[k], (place(other, z, x_lo), t))

    def sum_y():
        for k in range(1, NY):
            landed(ar2.at[k - 1], arecv_sem.at[k])
        arw[ar_rows(x_lo, y)] = arw[ar_rows(x_lo, y)] + ar2[0] + ar2[1] + ar2[2]
        for k in range(1, NZ):
            other = (z + k) % NZ
            send_now(arw.at[ar_rows(x_lo, y, other)], ar3.at[k - 1], asend_sem.at[3 + k], arecv_sem.at[3 + k], (place(y, other, x_lo), t))

    def sum_z():
        for k in range(1, NZ):
            landed(ar3.at[k - 1], arecv_sem.at[3 + k])
        total = arw[ar_rows(x_lo, y, z)]
        for k in range(NZ - 1):
            total = total + ar3[k]
        arg[ar_rows(x_lo, y, z)] = total
        for k in range(1, NZ):
            mine = arg.at[ar_rows(x_lo, y, z)]
            send_now(mine, mine, asend_sem.at[10 + k], arecv_sem.at[10 + k], (place(y, z + k, x_lo), t))

    def spread_y():
        for k in range(1, NZ):
            landed(ar3.at[0], arecv_sem.at[10 + k])
        for k in range(1, NY):
            mine = arg.at[ar_rows(x_lo, y)]
            send_now(mine, mine, asend_sem.at[17 + k], arecv_sem.at[17 + k], (place(y + k, z, x_lo), t))

    def spread_x():
        for k in range(1, NY):
            landed(ar2.at[0], arecv_sem.at[17 + k])
        mine = arg.at[ar_rows(x_lo)]
        send_now(mine, mine, asend_sem.at[21], arecv_sem.at[21], mate)

    def adapter_outputs():
        landed(ar1, arecv_sem.at[21])
        at = 0
        for j in range(owned_width // 128):
            down_out[:, j * 128 : (j + 1) * 128] = arg[at : at + rank3]
            at += rank3
        for ref in (upq_out, upk_out, upv_out):
            for j in range(ref.shape[1] // 128):
                ref[:, j * 128 : (j + 1) * 128] = arg[at : at + rank]
                at += rank

    def columns_ready():
        gain_column[...] = jnp.transpose(jnp.broadcast_to(gain_row, (128, owned_width)))
        for j in range(owned_width // 128):
            tok_t[j * 128 : (j + 1) * 128] = jnp.transpose(tok[:, j * 128 : (j + 1) * 128].astype(f32))

    def adapter_term():
        acc[...] = adapter_scale * lax.dot_general(
            jnp.transpose(down.astype(f32)).astype(bf16), out_low_buf[...], (((1,), (0,)), ((), ())), preferred_element_type=f32
        )

    starts = [sum(CHUNKS[:k]) for k in range(len(CHUNKS))]
    core_copies = {}
    same = x_lo == core
    my_chip = x_hi * 2 + x_lo

    def multiply(k):
        begin, count = starts[k], CHUNKS[k]
        lines = wbuf[begin : begin + count].reshape(count * SLOT, wbuf.shape[2])
        product = dot_nt(lines, gbuf[...])
        keep[begin * SLOT : (begin + count) * SLOT, :] = product[:, :tokens]
        csend[begin : begin + count] = product[:, tokens:].astype(bf16).reshape(count, SLOT, tokens)
        both = pl.ds(begin, count)
        core_copies[k] = send_now(csend.at[both], crecv.at[both], csend_sem.at[k], crecv_sem.at[k], twin)

    def pass_on(k):
        begin, count = starts[k], CHUNKS[k]
        core_copies[k].wait_recv()
        got = crecv[begin : begin + count].reshape(count * SLOT, tokens).astype(f32)
        total = keep[begin * SLOT : (begin + count) * SLOT, :] + got
        xs[begin : begin + count] = total.astype(bf16).reshape(count, SLOT, tokens)
        for slot in range(begin, begin + count):
            part, dy, dz = where[slot]
            owner_y, owner_z = (y + NY - dy) % NY, (z + NZ - dz) % NZ
            src = xs.at[slot, pl.ds(0, rows[part])]
            dst = xr.at[my_chip, owner_z, pl.ds(part * rows[0], rows[part])]
            own = jnp.logical_and(same, owner_y == t)

            @pl.when(own)
            def _():
                pltpu.make_async_copy(src, dst, xrecv_sem.at[my_chip]).start()

            @pl.when(jnp.logical_not(own))
            def _():
                remote(src, dst, xsend_sem, xrecv_sem.at[my_chip], (place(y, z, core), owner_y)).start()

    TASKS = {
        -1: (functools.partial(g_send, 0), low_products),
        1: (low_pair, functools.partial(g_send, 1)),
        8: (low_all, functools.partial(g_send, 2)),
        9: (columns_ready,),
        10: (functools.partial(g_send, 3), adapter_term),
        21: (sum_x,),
        29: (sum_y,),
        37: (sum_z,),
        45: (spread_y,),
        53: (spread_x,),
    }

    for task in TASKS[-1]:
        task()
    done_slots, done_chunks, passed = 2, 0, 0
    have = {(0, 0, 0, None), (1, 0, 0, None)}
    g_waited = False
    for index, (item, onward) in enumerate(log):
        landed(block(slots[item[:3]], item[0], item[3]), wrecv_sem.at[index])
        have.add(item)
        for link, new in onward:
            forward(item, link, new)
        if item[3] is None or (*item[:3], 1 - item[3]) in have:
            done_slots += 1
        for task in TASKS.get(index, ()):
            task()
        while done_chunks < len(CHUNKS) and starts[done_chunks] + CHUNKS[done_chunks] <= done_slots and index >= G_EVENT:
            if not g_waited:
                g_wait()
                g_waited = True
            multiply(done_chunks)
            done_chunks += 1
            if done_chunks - passed > 1:
                pass_on(passed)
                passed += 1
            if index < len(log) - 1:
                break
    while passed < len(CHUNKS):
        pass_on(passed)
        passed += 1
    adapter_outputs()
    for chip in range(4):
        landed(xr.at[chip], xrecv_sem.at[chip])

    inverse_row = inverse[:1]
    inner = jnp.zeros((8, tokens), f32)
    for owner_z in range(NZ):
        for half in range(2):
            begin = (owner_z * 2 + half) * (rows[0] + rows[1])
            lines = pl.ds(begin, rows[0] + rows[1])
            back = xr[half, owner_z].astype(f32) + xr[2 + half, owner_z].astype(f32) + acc[lines]
            gained = gain_column[lines, :1] * back
            acc[lines] = gained
            product = gained * (tok_t[lines] * inverse_row)
            inner = inner + product.reshape(-1, 8, tokens).sum(axis=0)
    inner_buf[0] = inner
    for k, device in enumerate((twin, across, (f, (1 - x_hi) * 2 + 1 - core))):
        send_now(inner_buf.at[0], inner_buf.at[k + 1], isend_sem.at[k], irecv_sem.at[k], device)
    for j in range(owned_width // 128):
        turned[:, j * 128 : (j + 1) * 128] = jnp.transpose(acc[j * 128 : (j + 1) * 128])
    for k in range(3):
        landed(inner_buf.at[k + 1], irecv_sem.at[k])
    total = (inner_buf[0] + inner_buf[1]) + (inner_buf[2] + inner_buf[3])
    total = jnp.sum(total, axis=0, keepdims=True) / full_width
    inner_column, inverse_column = as_column(total), as_column(inverse_row)
    unit = tok[...].astype(f32) * inverse_column
    grad[...] = (inverse_column * (turned[...] - unit * inner_column)).astype(bf16)

    for copy in started:
        copy.wait_send()

    @pl.when(same)
    def _():
        landed(xr.at[pl.ds(0, 3)], xsend_sem)

    @pl.when(jnp.logical_not(same))
    def _():
        landed(xr, xsend_sem)


def layer(weights, cotangents, tokens, gain, down, ups):
    count, owned_width = tokens.shape
    owned = weights[0].shape[0]
    rows = (40, owned - 40)
    width = sum(w.shape[1] for w in weights)
    events = len(gather_plan(rows)[1])
    slots = 2 * NY * NZ
    chunks = len(CHUNKS)
    rank3 = down.shape[0]
    f32, bf16, dma = jnp.float32, jnp.bfloat16, pltpu.SemaphoreType.DMA
    vmem = pl.BlockSpec(memory_space=pltpu.VMEM)
    return pl.pallas_call(
        functools.partial(layer_kernel, rows),
        out_shape=(
            jax.ShapeDtypeStruct((count, owned_width), bf16),
            jax.ShapeDtypeStruct((rank3, owned_width), f32),
            *(jax.ShapeDtypeStruct(u.shape, f32) for u in ups),
        ),
        in_specs=[pl.BlockSpec(memory_space=pl.ANY)] * 7 + [vmem] * 5,
        out_specs=(vmem,) * 5,
        scratch_shapes=[
            pltpu.VMEM((slots, SLOT, width), bf16),
            pltpu.VMEM((2 * count, width), bf16),
            pltpu.VMEM((slots * SLOT, count), f32),
            pltpu.VMEM((slots, SLOT, count), bf16),
            pltpu.VMEM((slots, SLOT, count), bf16),
            pltpu.VMEM((slots, SLOT, count), bf16),
            pltpu.VMEM((4, NZ, owned, count), bf16),
            pltpu.VMEM((count, owned_width), bf16),
            pltpu.VMEM((owned_width, count), f32),
            pltpu.VMEM((owned_width, count), f32),
            pltpu.VMEM((count, owned_width), f32),
            pltpu.VMEM((owned_width, 128), f32),
            pltpu.VMEM((4, 2 * rank3 + 8, count), f32),
            pltpu.VMEM((2 * rank3 + 8, count), f32),
            pltpu.VMEM((rank3, count), bf16),
            pltpu.VMEM((8, count), f32),
            pltpu.VMEM((4, 8, count), f32),
            pltpu.VMEM((1024, 128), f32),
            pltpu.VMEM((512, 128), f32),
            pltpu.VMEM((3, 128, 128), f32),
            pltpu.VMEM((7, 16, 128), f32),
            pltpu.VMEM((1024, 128), f32),
            dma((10,)), dma((events,)), dma((events,)), dma((G_PIECES,)), dma((G_PIECES,)),
            dma((chunks,)), dma((chunks,)), dma, dma((4,)),
            dma((2,)), dma((2,)), dma((22,)), dma((22,)), dma((3,)), dma((3,)),
        ],
        compiler_params=pltpu.CompilerParams(collective_id=0, has_side_effects=True, vmem_limit_bytes=60 << 20),
        cost_estimate=pl.CostEstimate(flops=9 * 10**9, bytes_accessed=6 * 10**6, transcendentals=0),
        name="layer",
    )(*weights, *cotangents, tokens, gain, down, *ups)


def shards(
    tokens,
    gain,
    query_projection_weight,
    key_projection_weight,
    value_projection_weight,
    adapter_down_factors,
    query_adapter_up,
    key_adapter_up,
    value_adapter_up,
    query_cotangent,
    key_cotangent,
    value_cotangent,
):
    kinds, rank, full_width = adapter_down_factors.shape
    grad_tokens, grad_down, *grad_ups = layer(
        (query_projection_weight, key_projection_weight, value_projection_weight),
        (query_cotangent, key_cotangent, value_cotangent),
        tokens,
        gain.reshape(1, full_width),
        adapter_down_factors.reshape(kinds * rank, full_width),
        (query_adapter_up, key_adapter_up, value_adapter_up),
    )
    return (grad_tokens, grad_down.reshape(kinds, rank, -1), *grad_ups)


def solution(mesh):
    in_specs = (
        P("fsdp", "tp"),
        P(),
        P("fsdp", "tp"),
        P("fsdp", "tp"),
        P("fsdp", "tp"),
        P(),
        P(None, "tp"),
        P(None, "tp"),
        P(None, "tp"),
        P("fsdp", "tp"),
        P("fsdp", "tp"),
        P("fsdp", "tp"),
    )
    out_specs = (P("fsdp", "tp"), P(None, None, "tp"), P(None, "tp"), P(None, "tp"), P(None, "tp"))
    return jax.shard_map(shards, mesh=mesh, in_specs=in_specs, out_specs=out_specs, check_vma=False)
```

time: 735 us -> 112 us (0.15)
  the two profiles are of different devices: /device:TPU:4 before, /device:TPU:1 now
where the time goes in v2:
time: 112 us; the launch traced here: 111 us
  Pallas kernels  104 us (93%)
  local copies, waits for them, and re-layouts  6.27 us (6%)
    pallas_call x1, Pallas kernels, layer(): pl.pallas_call(functools.partial(layer_kernel, rows), out_shape=(jax.Shap...  104 us
    unnamed x13, local copies, waits for them, and re-layouts  4.91 us

profile of v2, /device:TPU:1, one launch (start us, length us, event | category | flops | bytes accessed | tf_op | source)
XLA Modules:
  0.0 111.4 jit_solution(13496694306291519895)
XLA Ops:
  0.6 1.4 %reshape.19.gain_all = f32[1,5632]{1,0:T(1,128)} reshape(f32[5632]{0:T(1024)} %param.13) | data formatting | bytes 45056 | tf_op jit(solution)/shard_map/reshape | solution.py:524
  2.0 104.4 %layer.1 = (bf16[384,1408]{1,0:T(8,128)(2,1)}, f32[48,1408]{1,0:T(8,128)}, f32[16,1536]{1,0:T(8,128)}, f32[16,256]{1,0:T(8,128)}, f32[16,256]{1,0:T(8,128)}) custom-call(bf16[88,1536]{1,0:T(8,128)(2,1)} %wq.1, bf16[88,256]{1,0:T(8,128)(2,1)} %wk.1, bf16[88,256]{1,0:T(8,128)(2,1)} %wv.1, bf16[384,1536]{1,0:T(8,128)(2,1)} %gq.1, bf16[384,256]{1,0:T(8,128)(2,1)} %gk.1, ...), custom_call_target="tpu_custom_call" | custom-call | flops 8999999488 | bytes 6000000 | tf_op jit(solution)/shard_map/layer/pallas_call | solution.py:463
  106.4 0.0 copy-start
  106.4 0.0 copy-start.1
  106.4 0.0 copy-start.3
  106.5 0.0 copy-start.2
  106.5 2.3 %copy.22 = bf16[384,1408]{1,0:T(8,128)(2,1)} copy(bf16[384,1408]{1,0:T(8,128)(2,1)} %get-tuple-element.20) | data formatting | bytes 2162688
  108.8 0.0 copy-done
  108.8 0.7 copy.23
  109.5 0.0 copy-done.1
  109.5 0.6 copy.24
  110.2 0.0 copy-done.3
  110.2 0.6 copy.25
  110.8 0.0 copy-done.2
  110.8 0.6 copy.26
Async XLA Ops:
  106.4 2.4 %copy-start = (f32[48,1408]{1,0:T(8,128)S(1)}, f32[48,1408]{1,0:T(8,128)}, u32[]{:S(2)}) copy-start(f32[48,1408]{1,0:T(8,128)} %get-tuple-element.11) | copy-start | bytes 811012
  106.4 3.1 %copy-start.1 = (f32[16,1536]{1,0:T(8,128)S(1)}, f32[16,1536]{1,0:T(8,128)}, u32[]{:S(2)}) copy-start(f32[16,1536]{1,0:T(8,128)} %get-tuple-element.22) | copy-start | bytes 294916
  106.4 3.7 %copy-start.3 = (f32[16,256]{1,0:T(8,128)S(1)}, f32[16,256]{1,0:T(8,128)}, u32[]{:S(2)}) copy-start(f32[16,256]{1,0:T(8,128)} %get-tuple-element.23) | copy-start | bytes 49156
  106.5 4.3 %copy-start.2 = (f32[16,256]{1,0:T(8,128)S(1)}, f32[16,256]{1,0:T(8,128)}, u32[]{:S(2)}) copy-start(f32[16,256]{1,0:T(8,128)} %get-tuple-element.24) | copy-start | bytes 49156

commit v3 on v2

--- a/solution.py
+++ b/solution.py
@@ -15,9 +15,13 @@
 MESH = pl.DeviceIdType.MESH
 NY, NZ = 4, 8
 SLOT = 48
-CHUNKS = (8, 8, 8, 8, 8, 8, 8, 4, 4)
-G_PIECES = 4
-G_EVENT = 33
+CHUNKS = (8, 8, 8, 8, 8, 8, 8, 6, 2)
+G_PIECES = 8
+G_TIME = 44.0
+AR_USED = 25
+OUT_PIECES = 4
+VMEM_LIMIT = 60 << 20
+MOVED = {(1, 2): ("y+", 0), (-1, -2): ("y-", 0)}
 
 
 def forwards(have, item):
@@ -34,12 +38,14 @@
             if half is None or (0, 2, 0, 1 - half) in have:
                 out += [("z+", (0, dy, 1, None)), ("z-", (0, dy, -1, None))]
         elif dz > 0:
-            if dz < 3 or (dz == 3 and dy in (0, 1)):
+            if (dy, dz + 1) not in MOVED and (dz < 3 or (dz == 3 and dy in (0, 1))):
                 out += [("z+", (0, dy, dz + 1, None))]
         elif dz > -3:
-            out += [("z-", (0, dy, dz - 1, None))]
+            if (dy, dz - 1) not in MOVED:
+                out += [("z-", (0, dy, dz - 1, None))]
         elif dy in (-1, 2):
             out += [("z-", (0, dy, 4, None))]
+        out += [(link, (0, my, mz, None)) for (my, mz), (link, at) in MOVED.items() if (at, mz) == (dy, dz)]
     elif dy == 0:
         if dz == 0:
             out += [("z+", (1, 0, 1, None)), ("z-", (1, 0, -1, None))]
@@ -56,15 +62,16 @@
     return out
 
 
-def gather_plan(rows, rate=44.0, latency=1.9):
+def make_plan(rows, tasks, rate=44.0, latency=1.9, per_slot=0.23, per_half=0.15):
     size = [r * 4.096 for r in rows]
+    starts = [sum(CHUNKS[:k]) for k in range(len(CHUNKS))]
     free = dict.fromkeys(("y+", "y-", "z+", "z-"), 0.0)
-    have, events, log = set(), [], []
+    have, events, actions, serial = set(), [], [], iter(range(1000))
 
     def issue(now, link, item):
         span = size[item[0]] * (1.0 if item[3] is None else 0.5) / rate
         free[link] = max(now, free[link]) + span
-        heapq.heappush(events, (free[link] + latency, len(log) + len(events), link, item))
+        heapq.heappush(events, (free[link] + latency, next(serial), item))
 
     first = []
     for item in ((0, 0, 0, None), (1, 0, 0, None)):
@@ -73,22 +80,70 @@
     first = [e for e in first if e[0][0] == "y"] + [e for e in reversed(first) if e[0][0] == "z"]
     for link, item in first:
         issue(0.0, link, item)
-    count = len(first)
-    while events:
-        now, _, link, item = heapq.heappop(events)
-        have.add(item)
-        onward = forwards(have, item)
-        log.append((now, item, onward))
-        for link, new in onward:
-            issue(now + 0.1, link, new)
     slots = {(0, 0, 0): 0, (1, 0, 0): 1}
-    whole = []
-    for index, (now, item, _) in enumerate(log):
-        key = item[:3]
-        if item[3] is None or (*key, 1 - item[3]) in [e[1] for e in log[:index]]:
-            slots[key] = len(slots)
-            whole.append(index)
-    return first, [(item, onward) for _, item, onward in log], slots
+    tasks, now, done, owed, waiting = list(tasks), 0.0, 0, [], []
+    ready = 0.0
+    while events or tasks or done < len(CHUNKS) or owed or waiting:
+        if events and events[0][0] <= now:
+            item = heapq.heappop(events)[2]
+            have.add(item)
+            onward = forwards(have, item)
+            now += 0.06
+            for link, new in onward:
+                issue(now, link, new)
+            if item[3] is None or (*item[:3], 1 - item[3]) in have:
+                slots[item[:3]] = len(slots)
+            actions.append(("event", item, onward))
+        elif tasks and ready <= now and (tasks[0][0] != "spread_z" or not events):
+            name, span, axis, load, wait = tasks.pop(0)
+            actions.append(("task", name, None))
+            now += span
+            ready = now
+            for link in (axis + "+", axis + "-") if axis else ():
+                free[link] = max(now, free[link]) + load
+                ready = max(ready, free[link])
+            ready += wait
+        elif now >= G_TIME and owed:
+            k = owed.pop(0)
+            actions.append(("multiply", k, "mate"))
+            now += per_half * CHUNKS[k]
+            waiting.append((k, "mate"))
+            if len(waiting) > 1:
+                actions.append(("pass", *waiting.pop(0)))
+                now += 0.1
+        elif done < len(CHUNKS) and starts[done] + CHUNKS[done] <= len(slots):
+            kind = "both" if now >= G_TIME - 2.0 else "own"
+            actions.append(("multiply", done, kind))
+            if kind == "own":
+                owed.append(done)
+            now += (per_half if kind == "own" else per_slot) * CHUNKS[done]
+            waiting.append((done, kind))
+            done += 1
+            if len(waiting) > 1:
+                actions.append(("pass", *waiting.pop(0)))
+                now += 0.2
+        elif waiting and (done == len(CHUNKS) or now < G_TIME):
+            actions.append(("pass", *waiting.pop(0)))
+            now += 0.2
+        else:
+            wake = [e[0] for e in events[:1]] + [ready] * (ready > now)
+            now = max(now, min(wake + ([G_TIME] if now < G_TIME else [])))
+    return first, actions, slots
+
+
+TASKS = (
+    ("low_products", 2.2, "", 0.0, 1.9),
+    ("low_pair", 0.1, "", 0.0, 5.9),
+    ("low_part", 0.1, "", 0.0, 1.6),
+    ("low_all", 0.8, "", 0.0, 0.5),
+    ("columns_ready", 0.6, "", 0.0, 0.5),
+    ("adapter_term", 0.7, "", 0.0, 6.5),
+    ("sum_x", 0.1, "y", 3.0, 4.0),
+    ("sum_y", 0.1, "z", 1.5, 4.5),
+    ("sum_z", 0.1, "", 0.0, 6.5),
+    ("spread_x", 0.1, "z", 3.0, 4.5),
+    ("spread_z", 0.1, "", 0.0, 0.0),
+)
 
 
 def dot_nt(a, b):
@@ -101,21 +156,22 @@
 
 def layer_kernel(
     rows, wq, wk, wv, gq, gk, gv, tokens_hbm, gain_all, down_all, uq, uk, uv,
-    grad, down_out, upq_out, upk_out, upv_out,
+    grad_out, adapter_out,
     wbuf, gbuf, keep, csend, crecv, xs, xr,
-    tok, tok_t, acc, turned, gain_column, low, low_total, out_low_buf, inverse, inner_buf,
+    tok, tok_t, acc, turned, grad_buf, gain_column, low, low_total, out_low_buf, inverse, inner_buf,
     arw, ar1, ar2, ar3, arg,
     load_sem, wsend_sem, wrecv_sem, gsend_sem, grecv_sem, csend_sem, crecv_sem, xsend_sem, xrecv_sem,
-    lsend_sem, lrecv_sem, asend_sem, arecv_sem, isend_sem, irecv_sem,
+    lsend_sem, lrecv_sem, asend_sem, arecv_sem, isend_sem, irecv_sem, store_sem,
 ):
     f = lax.axis_index("fsdp")
     t = lax.axis_index("tp")
     y, z, x_lo = f // 16, (f // 2) % 8, f % 2
     x_hi, core = t // 2, t % 2
     tokens, owned_width = tokens_hbm.shape
-    full_width = gain_all.shape[1]
+    full_width = down_all.shape[1]
     f32, bf16 = jnp.float32, jnp.bfloat16
-    first, log, slots = gather_plan(rows)
+    first, actions, slots = make_plan(rows, TASKS)
+    log = [(item, onward) for kind, item, onward in actions if kind == "event"]
     where = {v: k for k, v in slots.items()}
 
     def place(yy, zz, xx):
@@ -199,7 +255,7 @@
     g_lines = tokens // G_PIECES
 
     def g_piece(k):
-        return gbuf.at[pl.ds(pl.multiple_of(own_half * tokens + k * g_lines, 32), g_lines)]
+        return gbuf.at[pl.ds(pl.multiple_of(own_half * tokens + k * g_lines, 16), g_lines)]
 
     def g_send(k):
         send_now(g_piece(k), g_piece(k), gsend_sem.at[k], grecv_sem.at[k], mate)
@@ -208,7 +264,8 @@
         for k in range(G_PIECES):
             landed(gbuf.at[pl.ds(0, g_lines)], grecv_sem.at[k])
 
-    gain_row = gain_all[:, pl.ds(pl.multiple_of(t * owned_width, 128), owned_width)]
+    gain_lines = gain_all[pl.ds(t * (owned_width // 128), owned_width // 128)]
+    gain_row = jnp.concatenate([gain_lines[k : k + 1] for k in range(owned_width // 128)], axis=1)
     down = down_all[:, pl.ds(pl.multiple_of(t * owned_width, 128), owned_width)]
     rank3, rank = down.shape[0], down.shape[0] // 3
 
@@ -231,19 +288,35 @@
         high = squares.astype(bf16)
         lowest = (squares - high.astype(f32)).astype(bf16)
         ones = jnp.ones((16, owned_width), bf16)
-        low[0, 2 * rank3 : 2 * rank3 + 8] = (dot_nt(ones, high) + dot_nt(ones, lowest))[:8]
+        low[0, 2 * rank3 :] = dot_nt(ones, high) + dot_nt(ones, lowest)
         send_now(low.at[0], low.at[1], lsend_sem.at[0], lrecv_sem.at[0], twin)
+
+    my_part = pl.ds(pl.multiple_of(core * (low_total.shape[0] // 2), 8), low_total.shape[0] // 2)
 
     def low_pair():
         landed(low.at[1], lrecv_sem.at[0])
         low[2] = low[0] + low[1]
-        send_now(low.at[2], low.at[3], lsend_sem.at[1], lrecv_sem.at[1], across)
+        send_now(low.at[2, my_part], low.at[3, my_part], lsend_sem.at[1], lrecv_sem.at[1], across)
+
+    def low_part():
+        landed(low.at[3, my_part], lrecv_sem.at[1])
+        low_total[my_part] = low[2, my_part] + low[3, my_part]
+        send_now(low_total.at[my_part], low_total.at[my_part], lsend_sem.at[2], lrecv_sem.at[2], twin)
 
     gradient_scale = adapter_scale / math.sqrt(tokens * 64)
 
+    used = AR_USED
+
+    class Lines:
+        at = 0
+
+    def pack(lines):
+        for k in range(lines.shape[0] // 16):
+            arw[Lines.at // 2, Lines.at % 2] = lines[k * 16 : (k + 1) * 16]
+            Lines.at += 1
+
     def low_all():
-        landed(low.at[3], lrecv_sem.at[1])
-        low_total[...] = low[2] + low[3]
+        landed(low_total.at[my_part], lrecv_sem.at[2])
         inverse_row = lax.rsqrt(low_total[2 * rank3 : 2 * rank3 + 8] / full_width + norm_eps)
         inverse[...] = inverse_row
         in_low = (low_total[0:rank3] * inverse_row[:1]).astype(bf16)
@@ -252,76 +325,62 @@
         unit = tok[...].astype(f32) * as_column(inverse_row[:1])
         normed = (unit * gain_row).astype(bf16)
         local = gradient_scale * jnp.dot(out_low, normed, preferred_element_type=f32)
-        at = 0
         for j in range(owned_width // 128):
-            arw[at : at + rank3] = local[:, j * 128 : (j + 1) * 128]
-            at += rank3
+            pack(local[:, j * 128 : (j + 1) * 128])
         for m in range(3):
             begin, width = spans[m]
             own = gbuf[pl.ds(own_begin, tokens), begin : begin + width]
             local = gradient_scale * jnp.dot(in_low[m * rank : (m + 1) * rank], own, preferred_element_type=f32)
             for j in range(width // 128):
-                arw[at : at + rank] = local[:, j * 128 : (j + 1) * 128]
-                at += rank
-        arw[at:] = jnp.zeros((arw.shape[0] - at, 128), f32)
-        send_now(arw.at[pl.ds(pl.multiple_of((1 - x_lo) * 512, 16), 512)], ar1, asend_sem.at[0], arecv_sem.at[0], mate)
-
-    def ar_rows(xx, yy=None, zz=None):
-        if yy is None:
-            return pl.ds(pl.multiple_of(xx * 512, 16), 512)
-        if zz is None:
-            return pl.ds(pl.multiple_of(xx * 512 + yy * 128, 16), 128)
-        return pl.ds(pl.multiple_of(xx * 512 + yy * 128 + zz * 16, 16), 16)
+                pack(local[:, j * 128 : (j + 1) * 128])
+        while Lines.at < 64:
+            pack(jnp.zeros((16, 128), f32))
+        send_now(arw.at[pl.ds(0, used), 1 - x_lo], ar1, asend_sem.at[0], arecv_sem.at[0], mate)
+
+    def of_y(yy):
+        return pl.ds(yy * NZ, NZ)
 
     def sum_x():
         landed(ar1, arecv_sem.at[0])
-        arw[ar_rows(x_lo)] = arw[ar_rows(x_lo)] + ar1[...]
+        arw[0:used, x_lo] = arw[0:used, x_lo] + ar1[...]
         for k in range(1, NY):
             other = (y + k) % NY
-            send_now(arw.at[ar_rows(x_lo, other)], ar2.at[k - 1], asend_sem.at[k], arecv_sem.at[k], (place(other, z, x_lo), t))
+            send_now(arw.at[of_y(other), x_lo], ar2.at[k - 1], asend_sem.at[k], arecv_sem.at[k], (place(other, z, x_lo), t))
 
     def sum_y():
         for k in range(1, NY):
             landed(ar2.at[k - 1], arecv_sem.at[k])
-        arw[ar_rows(x_lo, y)] = arw[ar_rows(x_lo, y)] + ar2[0] + ar2[1] + ar2[2]
+        arw[of_y(y), x_lo] = arw[of_y(y), x_lo] + ar2[0] + ar2[1] + ar2[2]
         for k in range(1, NZ):
             other = (z + k) % NZ
-            send_now(arw.at[ar_rows(x_lo, y, other)], ar3.at[k - 1], asend_sem.at[3 + k], arecv_sem.at[3 + k], (place(y, other, x_lo), t))
+            send_now(arw.at[y * NZ + other, x_lo], ar3.at[k - 1], asend_sem.at[3 + k], arecv_sem.at[3 + k], (place(y, other, x_lo), t))
 
     def sum_z():
         for k in range(1, NZ):
             landed(ar3.at[k - 1], arecv_sem.at[3 + k])
-        total = arw[ar_rows(x_lo, y, z)]
+        total = arw[y * NZ + z, x_lo]
         for k in range(NZ - 1):
             total = total + ar3[k]
-        arg[ar_rows(x_lo, y, z)] = total
+        arg[y * NZ + z, x_lo] = total
+        mine = arg.at[y * NZ + z, x_lo]
+        send_now(mine, mine, asend_sem.at[21], arecv_sem.at[21], mate)
+
+    def spread_x():
+        landed(ar3.at[0], arecv_sem.at[21])
         for k in range(1, NZ):
-            mine = arg.at[ar_rows(x_lo, y, z)]
+            mine = arg.at[y * NZ + z]
             send_now(mine, mine, asend_sem.at[10 + k], arecv_sem.at[10 + k], (place(y, z + k, x_lo), t))
 
+    def spread_z():
+        for k in range(1, NZ):
+            landed(arg.at[0], arecv_sem.at[10 + k])
+        for k in range(1, NY):
+            mine = arg.at[of_y(y)]
+            send_now(mine, mine, asend_sem.at[17 + k], arecv_sem.at[17 + k], (place(y + k, z, x_lo), t))
+
     def spread_y():
-        for k in range(1, NZ):
-            landed(ar3.at[0], arecv_sem.at[10 + k])
         for k in range(1, NY):
-            mine = arg.at[ar_rows(x_lo, y)]
-            send_now(mine, mine, asend_sem.at[17 + k], arecv_sem.at[17 + k], (place(y + k, z, x_lo), t))
-
-    def spread_x():
-        for k in range(1, NY):
-            landed(ar2.at[0], arecv_sem.at[17 + k])
-        mine = arg.at[ar_rows(x_lo)]
-        send_now(mine, mine, asend_sem.at[21], arecv_sem.at[21], mate)
-
-    def adapter_outputs():
-        landed(ar1, arecv_sem.at[21])
-        at = 0
-        for j in range(owned_width // 128):
-            down_out[:, j * 128 : (j + 1) * 128] = arg[at : at + rank3]
-            at += rank3
-        for ref in (upq_out, upk_out, upv_out):
-            for j in range(ref.shape[1] // 128):
-                ref[:, j * 128 : (j + 1) * 128] = arg[at : at + rank]
-                at += rank
+            landed(arg.at[pl.ds(0, NZ)], arecv_sem.at[17 + k])
 
     def columns_ready():
         gain_column[...] = jnp.transpose(jnp.broadcast_to(gain_row, (128, owned_width)))
@@ -334,22 +393,49 @@
         )
 
     starts = [sum(CHUNKS[:k]) for k in range(len(CHUNKS))]
-    core_copies = {}
     same = x_lo == core
     my_chip = x_hi * 2 + x_lo
 
-    def multiply(k):
+    def lines_of(k):
+        return wbuf[starts[k] : starts[k] + CHUNKS[k]].reshape(CHUNKS[k] * SLOT, wbuf.shape[2])
+
+    def hold(k, product):
+        keep[starts[k] * SLOT : (starts[k] + CHUNKS[k]) * SLOT, :] = product
+
+    def to_twin(k, product):
+        both = pl.ds(starts[k], CHUNKS[k])
+        csend[starts[k] : starts[k] + CHUNKS[k]] = product.astype(bf16).reshape(CHUNKS[k], SLOT, tokens)
+        return remote(csend.at[both], crecv.at[both], csend_sem.at[k], crecv_sem.at[k], twin)
+
+    def keeps(kind):
+        return same if kind == "own" else jnp.logical_not(same)
+
+    def multiply(k, kind):
+        if kind == "both":
+            product = dot_nt(lines_of(k), gbuf[...])
+            hold(k, product[:, :tokens])
+            to_twin(k, product[:, tokens:]).start()
+            return
+        half = own_half if kind == "own" else 1 - own_half
+        product = dot_nt(lines_of(k), gbuf[pl.ds(pl.multiple_of(half * tokens, 128), tokens)])
+
+        @pl.when(keeps(kind))
+        def _():
+            hold(k, product)
+
+        @pl.when(jnp.logical_not(keeps(kind)))
+        def _():
+            to_twin(k, product).start()
+
+    def pass_on(k, kind):
+        if kind == "both":
+            pass_lines(k)
+        else:
+            pl.when(keeps(kind))(functools.partial(pass_lines, k))
+
+    def pass_lines(k):
         begin, count = starts[k], CHUNKS[k]
-        lines = wbuf[begin : begin + count].reshape(count * SLOT, wbuf.shape[2])
-        product = dot_nt(lines, gbuf[...])
-        keep[begin * SLOT : (begin + count) * SLOT, :] = product[:, :tokens]
-        csend[begin : begin + count] = product[:, tokens:].astype(bf16).reshape(count, SLOT, tokens)
-        both = pl.ds(begin, count)
-        core_copies[k] = send_now(csend.at[both], crecv.at[both], csend_sem.at[k], crecv_sem.at[k], twin)
-
-    def pass_on(k):
-        begin, count = starts[k], CHUNKS[k]
-        core_copies[k].wait_recv()
+        landed(crecv.at[pl.ds(begin, count)], crecv_sem.at[k])
         got = crecv[begin : begin + count].reshape(count * SLOT, tokens).astype(f32)
         total = keep[begin * SLOT : (begin + count) * SLOT, :] + got
         xs[begin : begin + count] = total.astype(bf16).reshape(count, SLOT, tokens)
@@ -368,48 +454,36 @@
             def _():
                 remote(src, dst, xsend_sem, xrecv_sem.at[my_chip], (place(y, z, core), owner_y)).start()
 
-    TASKS = {
-        -1: (functools.partial(g_send, 0), low_products),
-        1: (low_pair, functools.partial(g_send, 1)),
-        8: (low_all, functools.partial(g_send, 2)),
-        9: (columns_ready,),
-        10: (functools.partial(g_send, 3), adapter_term),
-        21: (sum_x,),
-        29: (sum_y,),
-        37: (sum_z,),
-        45: (spread_y,),
-        53: (spread_x,),
+    g_send(0)
+    tasks = {
+        "low_products": (low_products,),
+        "low_pair": (low_pair, functools.partial(g_send, 1), functools.partial(g_send, 2)),
+        "low_part": (low_part,),
+        "low_all": (low_all, *(functools.partial(g_send, k) for k in range(3, G_PIECES))),
+        "columns_ready": (columns_ready,),
+        "adapter_term": (adapter_term,),
+        "sum_x": (sum_x,),
+        "sum_y": (sum_y,),
+        "sum_z": (sum_z,),
+        "spread_x": (spread_x,),
+        "spread_z": (spread_z,),
     }
-
-    for task in TASKS[-1]:
-        task()
-    done_slots, done_chunks, passed = 2, 0, 0
-    have = {(0, 0, 0, None), (1, 0, 0, None)}
-    g_waited = False
-    for index, (item, onward) in enumerate(log):
-        landed(block(slots[item[:3]], item[0], item[3]), wrecv_sem.at[index])
-        have.add(item)
-        for link, new in onward:
-            forward(item, link, new)
-        if item[3] is None or (*item[:3], 1 - item[3]) in have:
-            done_slots += 1
-        for task in TASKS.get(index, ()):
-            task()
-        while done_chunks < len(CHUNKS) and starts[done_chunks] + CHUNKS[done_chunks] <= done_slots and index >= G_EVENT:
-            if not g_waited:
+    g_here = False
+    for kind, what, onward in actions:
+        if kind == "event":
+            landed(block(slots[what[:3]], what[0], what[3]), wrecv_sem.at[event_index[what]])
+            for link, new in onward:
+                forward(what, link, new)
+        elif kind == "task":
+            for task in tasks[what]:
+                task()
+        elif kind == "multiply":
+            if onward != "own" and not g_here:
                 g_wait()
-                g_waited = True
-            multiply(done_chunks)
-            done_chunks += 1
-            if done_chunks - passed > 1:
-                pass_on(passed)
-                passed += 1
-            if index < len(log) - 1:
-                break
-    while passed < len(CHUNKS):
-        pass_on(passed)
-        passed += 1
-    adapter_outputs()
+                g_here = True
+            multiply(what, onward)
+        else:
+            pass_on(what, onward)
     for chip in range(4):
         landed(xr.at[chip], xrecv_sem.at[chip])
 
@@ -429,17 +503,27 @@
         send_now(inner_buf.at[0], inner_buf.at[k + 1], isend_sem.at[k], irecv_sem.at[k], device)
     for j in range(owned_width // 128):
         turned[:, j * 128 : (j + 1) * 128] = jnp.transpose(acc[j * 128 : (j + 1) * 128])
+    inverse_column = as_column(inverse_row)
+    spread_y()
+    stores = [pltpu.make_async_copy(arg.at[pl.ds(0, used)], adapter_out, store_sem.at[0])]
+    stores[0].start()
     for k in range(3):
         landed(inner_buf.at[k + 1], irecv_sem.at[k])
     total = (inner_buf[0] + inner_buf[1]) + (inner_buf[2] + inner_buf[3])
-    total = jnp.sum(total, axis=0, keepdims=True) / full_width
-    inner_column, inverse_column = as_column(total), as_column(inverse_row)
-    unit = tok[...].astype(f32) * inverse_column
-    grad[...] = (inverse_column * (turned[...] - unit * inner_column)).astype(bf16)
-
+    inner_column = as_column(jnp.sum(total, axis=0, keepdims=True) / full_width)
+    step = tokens // OUT_PIECES
+    for k in range(OUT_PIECES):
+        lines = slice(k * step, (k + 1) * step)
+        scale = inverse_column[lines]
+        unit = tok[lines].astype(f32) * scale
+        grad_buf[lines] = (scale * (turned[lines] - unit * inner_column[lines])).astype(bf16)
+        stores.append(pltpu.make_async_copy(grad_buf.at[pl.ds(k * step, step)], grad_out.at[pl.ds(k * step, step)], store_sem.at[1 + k]))
+        stores[-1].start()
     for copy in started:
         copy.wait_send()
-
+    for k in range(len(CHUNKS)):
+        both = pl.ds(starts[k], CHUNKS[k])
+        landed(csend.at[both], csend_sem.at[k])
     @pl.when(same)
     def _():
         landed(xr.at[pl.ds(0, 3)], xsend_sem)
@@ -447,6 +531,9 @@
     @pl.when(jnp.logical_not(same))
     def _():
         landed(xr, xsend_sem)
+
+    for copy in stores:
+        copy.wait()
 
 
 def layer(weights, cotangents, tokens, gain, down, ups):
@@ -454,7 +541,7 @@
     owned = weights[0].shape[0]
     rows = (40, owned - 40)
     width = sum(w.shape[1] for w in weights)
-    events = len(gather_plan(rows)[1])
+    events = sum(kind == "event" for kind, _, _ in make_plan(rows, TASKS)[1])
     slots = 2 * NY * NZ
     chunks = len(CHUNKS)
     rank3 = down.shape[0]
@@ -464,11 +551,10 @@
         functools.partial(layer_kernel, rows),
         out_shape=(
             jax.ShapeDtypeStruct((count, owned_width), bf16),
-            jax.ShapeDtypeStruct((rank3, owned_width), f32),
-            *(jax.ShapeDtypeStruct(u.shape, f32) for u in ups),
+            jax.ShapeDtypeStruct((AR_USED, 2, 16, 128), f32),
         ),
         in_specs=[pl.BlockSpec(memory_space=pl.ANY)] * 7 + [vmem] * 5,
-        out_specs=(vmem,) * 5,
+        out_specs=(pl.BlockSpec(memory_space=pl.ANY),) * 2,
         scratch_shapes=[
             pltpu.VMEM((slots, SLOT, width), bf16),
             pltpu.VMEM((2 * count, width), bf16),
@@ -481,25 +567,55 @@
             pltpu.VMEM((owned_width, count), f32),
             pltpu.VMEM((owned_width, count), f32),
             pltpu.VMEM((count, owned_width), f32),
+            pltpu.VMEM((count, owned_width), bf16),
             pltpu.VMEM((owned_width, 128), f32),
-            pltpu.VMEM((4, 2 * rank3 + 8, count), f32),
-            pltpu.VMEM((2 * rank3 + 8, count), f32),
+            pltpu.VMEM((4, 2 * rank3 + 16, count), f32),
+            pltpu.VMEM((2 * rank3 + 16, count), f32),
             pltpu.VMEM((rank3, count), bf16),
             pltpu.VMEM((8, count), f32),
             pltpu.VMEM((4, 8, count), f32),
-            pltpu.VMEM((1024, 128), f32),
-            pltpu.VMEM((512, 128), f32),
-            pltpu.VMEM((3, 128, 128), f32),
-            pltpu.VMEM((7, 16, 128), f32),
-            pltpu.VMEM((1024, 128), f32),
+            pltpu.VMEM((NY * NZ, 2, 16, 128), f32),
+            pltpu.VMEM((AR_USED, 16, 128), f32),
+            pltpu.VMEM((NY - 1, NZ, 16, 128), f32),
+            pltpu.VMEM((NZ - 1, 16, 128), f32),
+            pltpu.VMEM((NY * NZ, 2, 16, 128), f32),
             dma((10,)), dma((events,)), dma((events,)), dma((G_PIECES,)), dma((G_PIECES,)),
             dma((chunks,)), dma((chunks,)), dma, dma((4,)),
-            dma((2,)), dma((2,)), dma((22,)), dma((22,)), dma((3,)), dma((3,)),
+            dma((3,)), dma((3,)), dma((22,)), dma((22,)), dma((3,)), dma((3,)), dma((1 + OUT_PIECES,)),
         ],
-        compiler_params=pltpu.CompilerParams(collective_id=0, has_side_effects=True, vmem_limit_bytes=60 << 20),
+        compiler_params=pltpu.CompilerParams(collective_id=0, has_side_effects=True, vmem_limit_bytes=VMEM_LIMIT),
         cost_estimate=pl.CostEstimate(flops=9 * 10**9, bytes_accessed=6 * 10**6, transcendentals=0),
         name="layer",
     )(*weights, *cotangents, tokens, gain, down, *ups)
+
+
+def finish_kernel(grad_in, adapter, grad, down, upq, upk, upv):
+    @pl.when(pl.program_id(0) == 0)
+    def _():
+        at = 0
+        for ref in (down, upq, upk, upv):
+            for j in range(ref.shape[1] // 128):
+                for k in range(ref.shape[0] // 16):
+                    ref[k * 16 : (k + 1) * 16, j * 128 : (j + 1) * 128] = adapter[at // 2, at % 2]
+                    at += 1
+
+    grad[...] = grad_in[...]
+
+
+def finish(grad, adapter, rank3, ups):
+    count, owned_width = grad.shape
+    steps = 4
+    f32 = jnp.float32
+    shapes = [(rank3, owned_width)] + [u.shape for u in ups]
+    block = pl.BlockSpec((count // steps, owned_width), lambda i: (i, 0))
+    return pl.pallas_call(
+        finish_kernel,
+        grid=(steps,),
+        out_shape=(jax.ShapeDtypeStruct(grad.shape, grad.dtype), *(jax.ShapeDtypeStruct(s, f32) for s in shapes)),
+        in_specs=[block, pl.BlockSpec(adapter.shape, lambda i: (0, 0, 0, 0))],
+        out_specs=(block, *(pl.BlockSpec(s, lambda i: (0, 0)) for s in shapes)),
+        name="finish",
+    )(grad, adapter)
 
 
 def shards(
@@ -517,14 +633,16 @@
     value_cotangent,
 ):
     kinds, rank, full_width = adapter_down_factors.shape
-    grad_tokens, grad_down, *grad_ups = layer(
+    ups = (query_adapter_up, key_adapter_up, value_adapter_up)
+    grad_tokens, adapter = layer(
         (query_projection_weight, key_projection_weight, value_projection_weight),
         (query_cotangent, key_cotangent, value_cotangent),
         tokens,
-        gain.reshape(1, full_width),
+        gain.reshape(-1, 128),
         adapter_down_factors.reshape(kinds * rank, full_width),
-        (query_adapter_up, key_adapter_up, value_adapter_up),
+        ups,
     )
+    grad_tokens, grad_down, *grad_ups = finish(grad_tokens, adapter, kinds * rank, ups)
     return (grad_tokens, grad_down.reshape(kinds, rank, -1), *grad_ups)
 
 

time: 112 us -> 100 us (0.89)
  local copies, waits for them, and re-layouts: 6.27 us -> 0 us
  Pallas kernels: 104 us -> 99.2 us
    pallas_call x1, Pallas kernels: 104 us -> 95.6 us  [layer(): pl.pallas_call(functools.partial(layer_kernel, rows), out_shape=(jax.Shap...]
    unnamed x13 -> x0, local copies, waits for them, and re-layouts: 4.91 us -> none
    pallas_call x0 -> x1, Pallas kernels: none -> 3.68 us  [finish(): pl.pallas_call(finish_kernel, grid=(steps,), out_shape=(jax.ShapeDtypeStr...]
    reshape x1 -> x0, local copies, waits for them, and re-layouts: 1.36 us -> none  [shards(): gain.reshape(1, full_width)]
where the time goes in v3:
time: 100 us
  Pallas kernels  99.2 us (99%)
    pallas_call x1, Pallas kernels, layer(): pl.pallas_call(functools.partial(layer_kernel, rows), out_shape=(jax.Shap...  95.6 us
    pallas_call x1, Pallas kernels, finish(): pl.pallas_call(finish_kernel, grid=(steps,), out_shape=(jax.ShapeDtypeStr...  3.68 us

profile of v3, /device:TPU:1, one launch (start us, length us, event | category | flops | bytes accessed | tf_op | source)
XLA Modules:
  0.0 100.0 jit_solution(12343127333718115778)
XLA Ops:
  0.6 95.6 %layer.1 = (bf16[384,1408]{1,0:T(8,128)(2,1)}, f32[25,2,16,128]{3,2,1,0:T(8,128)}) custom-call(bf16[88,1536]{1,0:T(8,128)(2,1)} %wq.1, bf16[88,256]{1,0:T(8,128)(2,1)} %wk.1, bf16[88,256]{1,0:T(8,128)(2,1)} %wv.1, bf16[384,1536]{1,0:T(8,128)(2,1)} %gq.1, bf16[384,256]{1,0:T(8,128)(2,1)} %gk.1, bf16[384,256]{1,0:T(8,128)(2,1)} %gv.1, ...), custom_call_target="tpu_custom_call" | custom-call | flops 8999999488 | bytes 6000000 | tf_op jit(solution)/shard_map/layer/pallas_call | solution.py:550
  96.2 3.7 %finish.1 = (bf16[384,1408]{1,0:T(8,128)(2,1)}, f32[48,1408]{1,0:T(8,128)}, f32[16,1536]{1,0:T(8,128)}, f32[16,256]{1,0:T(8,128)}, f32[16,256]{1,0:T(8,128)}) custom-call(bf16[384,1408]{1,0:T(8,128)(2,1)} %get-tuple-element.12.grad_in, f32[25,2,16,128]{3,2,1,0:T(8,128)} %get-tuple-element.13.adapter), custom_call_target="tpu_custom_call" | custom-call | tf_op jit(solution)/shard_map/finish/pallas_call | solution.py:611

commit v4 on v3

--- a/solution.py
+++ b/solution.py
@@ -15,12 +15,13 @@
 MESH = pl.DeviceIdType.MESH
 NY, NZ = 4, 8
 SLOT = 48
-CHUNKS = (8, 8, 8, 8, 8, 8, 8, 6, 2)
+CHUNKS = (8, 8, 8, 8, 8, 8, 4, 4, 3, 3, 2)
 G_PIECES = 8
 G_TIME = 44.0
+LAST = ("spread_x", "spread_z")
 AR_USED = 25
 OUT_PIECES = 4
-VMEM_LIMIT = 60 << 20
+VMEM_LIMIT = 50 << 20
 MOVED = {(1, 2): ("y+", 0), (-1, -2): ("y-", 0)}
 
 
@@ -62,7 +63,7 @@
     return out
 
 
-def make_plan(rows, tasks, rate=44.0, latency=1.9, per_slot=0.23, per_half=0.15):
+def make_plan(rows, tasks, rate=44.0, latency=1.9, per_slot=0.23, per_half=0.13, twin=2.6):
     size = [r * 4.096 for r in rows]
     starts = [sum(CHUNKS[:k]) for k in range(len(CHUNKS))]
     free = dict.fromkeys(("y+", "y-", "z+", "z-"), 0.0)
@@ -94,7 +95,7 @@
             if item[3] is None or (*item[:3], 1 - item[3]) in have:
                 slots[item[:3]] = len(slots)
             actions.append(("event", item, onward))
-        elif tasks and ready <= now and (tasks[0][0] != "spread_z" or not events):
+        elif tasks and ready <= now and (tasks[0][0] not in LAST or not events):
             name, span, axis, load, wait = tasks.pop(0)
             actions.append(("task", name, None))
             now += span
@@ -103,30 +104,24 @@
                 free[link] = max(now, free[link]) + load
                 ready = max(ready, free[link])
             ready += wait
+        elif waiting and waiting[0][0] <= now:
+            actions.append(("pass", *waiting.pop(0)[1:]))
+            now += 0.3
         elif now >= G_TIME and owed:
             k = owed.pop(0)
             actions.append(("multiply", k, "mate"))
             now += per_half * CHUNKS[k]
-            waiting.append((k, "mate"))
-            if len(waiting) > 1:
-                actions.append(("pass", *waiting.pop(0)))
-                now += 0.1
+            waiting.append((now + twin, k, "mate"))
         elif done < len(CHUNKS) and starts[done] + CHUNKS[done] <= len(slots):
             kind = "both" if now >= G_TIME - 2.0 else "own"
             actions.append(("multiply", done, kind))
             if kind == "own":
                 owed.append(done)
             now += (per_half if kind == "own" else per_slot) * CHUNKS[done]
-            waiting.append((done, kind))
+            waiting.append((now + twin, done, kind))
             done += 1
-            if len(waiting) > 1:
-                actions.append(("pass", *waiting.pop(0)))
-                now += 0.2
-        elif waiting and (done == len(CHUNKS) or now < G_TIME):
-            actions.append(("pass", *waiting.pop(0)))
-            now += 0.2
         else:
-            wake = [e[0] for e in events[:1]] + [ready] * (ready > now)
+            wake = [e[0] for e in events[:1]] + [e[0] for e in waiting[:1]] + [ready] * (ready > now)
             now = max(now, min(wake + ([G_TIME] if now < G_TIME else [])))
     return first, actions, slots
 
@@ -155,10 +150,10 @@
 
 
 def layer_kernel(
-    rows, wq, wk, wv, gq, gk, gv, tokens_hbm, gain_all, down_all, uq, uk, uv,
+    rows, wq, wk, wv, gq, gk, gv, tokens_hbm, gain_hbm, down_hbm, uq_hbm, uk_hbm, uv_hbm,
     grad_out, adapter_out,
     wbuf, gbuf, keep, csend, crecv, xs, xr,
-    tok, tok_t, acc, turned, grad_buf, gain_column, low, low_total, out_low_buf, inverse, inner_buf,
+    gain_all, down_all, uq, uk, uv, tok, tok_t, acc, turned, grad_buf, gain_column, low, low_total, out_low_buf, inverse, inner_buf,
     arw, ar1, ar2, ar3, arg,
     load_sem, wsend_sem, wrecv_sem, gsend_sem, grecv_sem, csend_sem, crecv_sem, xsend_sem, xrecv_sem,
     lsend_sem, lrecv_sem, asend_sem, arecv_sem, isend_sem, irecv_sem, store_sem,
@@ -219,6 +214,10 @@
         loads.append(pltpu.make_async_copy(g, gbuf.at[pl.ds(own_begin, tokens), columns], load_sem.at[3 * index + 2]))
     for load in loads:
         load.start()
+    small = ((gain_hbm, gain_all), (down_hbm, down_all), (uq_hbm, uq), (uk_hbm, uk), (uv_hbm, uv))
+    for index, (src, dst) in enumerate(small):
+        loads.append(pltpu.make_async_copy(src, dst, load_sem.at[10 + index]))
+        loads[-1].start()
     token_load.start()
 
     barrier = pltpu.get_barrier_semaphore()
@@ -546,14 +545,13 @@
     chunks = len(CHUNKS)
     rank3 = down.shape[0]
     f32, bf16, dma = jnp.float32, jnp.bfloat16, pltpu.SemaphoreType.DMA
-    vmem = pl.BlockSpec(memory_space=pltpu.VMEM)
     return pl.pallas_call(
         functools.partial(layer_kernel, rows),
         out_shape=(
             jax.ShapeDtypeStruct((count, owned_width), bf16),
             jax.ShapeDtypeStruct((AR_USED, 2, 16, 128), f32),
         ),
-        in_specs=[pl.BlockSpec(memory_space=pl.ANY)] * 7 + [vmem] * 5,
+        in_specs=[pl.BlockSpec(memory_space=pltpu.HBM)] * 12,
         out_specs=(pl.BlockSpec(memory_space=pl.ANY),) * 2,
         scratch_shapes=[
             pltpu.VMEM((slots, SLOT, width), bf16),
@@ -563,6 +561,7 @@
             pltpu.VMEM((slots, SLOT, count), bf16),
             pltpu.VMEM((slots, SLOT, count), bf16),
             pltpu.VMEM((4, NZ, owned, count), bf16),
+            *(pltpu.VMEM(a.shape, a.dtype) for a in (gain, down, *ups)),
             pltpu.VMEM((count, owned_width), bf16),
             pltpu.VMEM((owned_width, count), f32),
             pltpu.VMEM((owned_width, count), f32),
@@ -579,41 +578,43 @@
             pltpu.VMEM((NY - 1, NZ, 16, 128), f32),
             pltpu.VMEM((NZ - 1, 16, 128), f32),
             pltpu.VMEM((NY * NZ, 2, 16, 128), f32),
-            dma((10,)), dma((events,)), dma((events,)), dma((G_PIECES,)), dma((G_PIECES,)),
+            dma((15,)), dma((events,)), dma((events,)), dma((G_PIECES,)), dma((G_PIECES,)),
             dma((chunks,)), dma((chunks,)), dma, dma((4,)),
             dma((3,)), dma((3,)), dma((22,)), dma((22,)), dma((3,)), dma((3,)), dma((1 + OUT_PIECES,)),
         ],
         compiler_params=pltpu.CompilerParams(collective_id=0, has_side_effects=True, vmem_limit_bytes=VMEM_LIMIT),
         cost_estimate=pl.CostEstimate(flops=9 * 10**9, bytes_accessed=6 * 10**6, transcendentals=0),
         name="layer",
-    )(*weights, *cotangents, tokens, gain, down, *ups)
-
-
-def finish_kernel(grad_in, adapter, grad, down, upq, upk, upv):
-    @pl.when(pl.program_id(0) == 0)
-    def _():
-        at = 0
-        for ref in (down, upq, upk, upv):
-            for j in range(ref.shape[1] // 128):
-                for k in range(ref.shape[0] // 16):
-                    ref[k * 16 : (k + 1) * 16, j * 128 : (j + 1) * 128] = adapter[at // 2, at % 2]
-                    at += 1
-
-    grad[...] = grad_in[...]
+    )(*(pltpu.with_memory_space_constraint(a, pltpu.HBM) for a in (*weights, *cotangents, tokens, gain, down, *ups)))
+
+
+def finish_kernel(grad_in, adapter_in, grad, down, upq, upk, upv, adapter, sem):
+    load = pltpu.make_async_copy(adapter_in, adapter, sem.at[0])
+    load.start()
+    store = pltpu.make_async_copy(grad_in, grad, sem.at[1])
+    store.start()
+    load.wait()
+    at = 0
+    for ref in (down, upq, upk, upv):
+        for j in range(ref.shape[1] // 128):
+            for k in range(ref.shape[0] // 16):
+                ref[k * 16 : (k + 1) * 16, j * 128 : (j + 1) * 128] = adapter[at // 2, at % 2]
+                at += 1
+    store.wait()
 
 
 def finish(grad, adapter, rank3, ups):
-    count, owned_width = grad.shape
-    steps = 4
     f32 = jnp.float32
-    shapes = [(rank3, owned_width)] + [u.shape for u in ups]
-    block = pl.BlockSpec((count // steps, owned_width), lambda i: (i, 0))
+    shapes = [(rank3, grad.shape[1])] + [u.shape for u in ups]
+    vmem = pl.BlockSpec(memory_space=pltpu.VMEM)
+    hbm = pl.BlockSpec(memory_space=pl.ANY)
     return pl.pallas_call(
         finish_kernel,
-        grid=(steps,),
         out_shape=(jax.ShapeDtypeStruct(grad.shape, grad.dtype), *(jax.ShapeDtypeStruct(s, f32) for s in shapes)),
-        in_specs=[block, pl.BlockSpec(adapter.shape, lambda i: (0, 0, 0, 0))],
-        out_specs=(block, *(pl.BlockSpec(s, lambda i: (0, 0)) for s in shapes)),
+        in_specs=[hbm, hbm],
+        out_specs=(hbm, *(vmem,) * 4),
+        scratch_shapes=[pltpu.VMEM(adapter.shape, f32), pltpu.SemaphoreType.DMA((2,))],
+        compiler_params=pltpu.CompilerParams(vmem_limit_bytes=16 << 20),
         name="finish",
     )(grad, adapter)
 

time: 100 us -> 93.4 us (0.934)
  Pallas kernels: 99.2 us -> 92.6 us
    pallas_call x1, Pallas kernels: 95.6 us -> 90.6 us  [layer(): pl.pallas_call(functools.partial(layer_kernel, rows), out_shape=(jax.Shap...]
    pallas_call x1, Pallas kernels: 3.68 us -> 1.95 us  [finish(): pl.pallas_call(finish_kernel, out_shape=(jax.ShapeDtypeStruct(grad.shape,...]
where the time goes in v4:
time: 93.4 us
  Pallas kernels  92.6 us (99%)
    pallas_call x1, Pallas kernels, layer(): pl.pallas_call(functools.partial(layer_kernel, rows), out_shape=(jax.Shap...  90.6 us
    pallas_call x1, Pallas kernels, finish(): pl.pallas_call(finish_kernel, out_shape=(jax.ShapeDtypeStruct(grad.shape,...  1.95 us

profile of v4, /device:TPU:1, one launch (start us, length us, event | category | flops | bytes accessed | tf_op | source)
XLA Modules:
  0.0 93.4 jit_solution(6003892847839834544)
XLA Ops:
  0.6 90.6 %layer.1 = (bf16[384,1408]{1,0:T(8,128)(2,1)S(1)}, f32[25,2,16,128]{3,2,1,0:T(8,128)S(1)}) custom-call(bf16[88,1536]{1,0:T(8,128)(2,1)} %wq.1, bf16[88,256]{1,0:T(8,128)(2,1)} %wk.1, bf16[88,256]{1,0:T(8,128)(2,1)} %wv.1, bf16[384,1536]{1,0:T(8,128)(2,1)} %gq.1, bf16[384,256]{1,0:T(8,128)(2,1)} %gk.1, bf16[384,256]{1,0:T(8,128)(2,1)} %gv.1, ...), custom_call_target="tpu_custom_call" | custom-call | flops 8999999488 | bytes 6000000 | tf_op jit(solution)/shard_map/layer/pallas_call | solution.py:548
  91.2 1.9 %finish.1 = (bf16[384,1408]{1,0:T(8,128)(2,1)}, f32[48,1408]{1,0:T(8,128)}, f32[16,1536]{1,0:T(8,128)}, f32[16,256]{1,0:T(8,128)}, f32[16,256]{1,0:T(8,128)}) custom-call(bf16[384,1408]{1,0:T(8,128)(2,1)S(1)} %get-tuple-element.12.grad_in, f32[25,2,16,128]{3,2,1,0:T(8,128)S(1)} %get-tuple-element.13.adapter_in), custom_call_target="tpu_custom_call" | custom-call | tf_op jit(solution)/shard_map/finish/pallas_call | solution.py:611
